TPU v7x, 128 devices: a whole 4x4x4 slice. The times are simulated.
128 devices in a mesh: dp: 32 (over x_lo, z, y), tr: 2 (over core), tc: 2 (over x_hi).
Axes of the slice: x: 4 (x_hi: 2, x_lo: 2; x = x_hi * 2 + x_lo), y: 4, z: 4, core: 2. Of those that a mesh axis runs over, the one named last changes fastest.
Arguments:
- activations: bfloat16 [16384, 4096], P('dp', ('tr', 'tc')), may hold values from -16.8 to 16.8, as said below
- gradients: bfloat16 [16384, 7168], P('dp', ('tr', 'tc')), may hold values from -16.8 to 16.8, as said below
- old_inputs: float32 [4096, 4096], P(('dp', 'tr', 'tc')), may hold values from -3 to 3
- old_gradients: float32 [7168, 7168], P(('dp', 'tr', 'tc')), may hold values from -3 to 3
Outputs:
- input_factor: float32 [4096, 4096], P(('dp', 'tr', 'tc'))
- grad_factor: float32 [7168, 7168], P(('dp', 'tr', 'tc'))
Inputs may be any that keep to these rules, and one draw needn't show every extreme that they name: `activations`: real-valued samples. `gradients`: real-valued samples.
All inputs are finite; a program needn't handle non-finite values.
Results may differ from a plain program's by a relative error of at most 0.0045.
Values may be sent and summed in bfloat16 or wider, within the bound.
A program may use at most 192 MiB of HBM per device.

v0:
```python
import jax
import jax.numpy as jnp
from jax import lax
from jax.sharding import Mesh
from jax.sharding import PartitionSpec as P

DP = ("dp_0", "dp_1", "dp_2")
DP_TR_TC = ("dp_0", "dp_1", "dp_2", "tr", "tc")


def own_block(blocks, axes, sequence):
    inside = blocks.shape[1:]
    blocks = blocks.reshape(*(lax.axis_size(a) for a in axes), *inside)
    blocks = jnp.moveaxis(blocks, sequence, range(len(axes))).reshape(-1, *inside)
    for k in sequence:
        blocks = lax.psum_scatter(blocks, axes[k], scatter_dimension=0, tiled=True)
    return blocks[0]


def in_blocks(value, dim, count):
    shape = value.shape
    blocks = value.reshape(*shape[:dim], count, shape[dim] // count, *shape[dim + 1 :])
    return jnp.moveaxis(blocks, dim, 0)


def sum_by_axis_2(value, axes, sequence, dim):
    count = lax.axis_size(axes)
    return own_block(in_blocks(value, dim, count), axes, sequence)


def select_rows(gathered, tensor_index, tensor_count, block_total, block_width):
    token_count = gathered.shape[0]
    blocks = gathered.reshape(token_count, -1, tensor_count, block_width)
    picked = lax.dynamic_index_in_dim(blocks, tensor_index, 2, keepdims=False)
    return picked.reshape(token_count, block_total * block_width)


def full_term(gathered, tensor_index, tensor_count, block_width, tokens_all, row_count):
    block_total = row_count // block_width
    left_rows = select_rows(gathered, tensor_index, tensor_count, block_total, block_width)
    product = lax.dot_general(
        left_rows, gathered, (((0,), (0,)), ((), ())), preferred_element_type=jnp.float32
    )
    return product / tokens_all


def body(activations, gradients, old_inputs, old_gradients):
    full_acts, full_grads = (
        lax.all_gather(activations, ("tr", "tc"), axis=1, tiled=True),
        lax.all_gather(gradients, ("tr", "tc"), axis=1, tiled=True),
    )
    tensor_count = lax.axis_size(("tr", "tc"))
    replicas = lax.axis_size(DP)
    tensor_index = lax.axis_index(("tr", "tc"))
    tokens_all = activations.shape[0] * replicas
    input_width = old_inputs.shape[0]
    grad_width = old_gradients.shape[0]
    input_new = sum_by_axis_2(
        full_term(
            full_acts,
            tensor_index,
            tensor_count,
            input_width,
            tokens_all,
            input_width * lax.axis_size(DP),
        ).astype(jnp.bfloat16),
        DP,
        (1, 2, 0),
        0,
    ).astype(jnp.float32)
    gradient_new = lax.psum_scatter(
        full_term(
            full_grads,
            tensor_index,
            tensor_count,
            grad_width,
            tokens_all,
            lax.axis_size(DP) * grad_width,
        ).astype(jnp.bfloat16),
        DP,
        scatter_dimension=0,
        tiled=True,
    ).astype(jnp.float32)
    return (0.5 * old_inputs + 0.5 * input_new, 0.5 * old_gradients + 0.5 * gradient_new)


def solution(mesh):
    finer = Mesh(
        mesh.devices.reshape(2, 4, 4, mesh.shape["tr"], mesh.shape["tc"]),
        ("dp_0", "dp_1", "dp_2", "tr", "tc"),
    )
    return jax.shard_map(
        body,
        mesh=finer,
        in_specs=(P(DP, ("tr", "tc")), P(DP, ("tr", "tc")), P(DP_TR_TC, None), P(DP_TR_TC, None)),
        out_specs=(P(DP_TR_TC, None), P(DP_TR_TC, None)),
        check_vma=False,
    )
```

profile of v0, /device:TPU:1, one launch (start us, length us, event | category | flops | bytes accessed | tf_op | source)
XLA Modules:
  0.0 554.0 jit_solution(9826447268660505543)
XLA Ops:
  7.2 0.0 all-gather.3.cloned.1.call-start
  7.2 2.3 copy.7
  9.5 0.0 all-gather.3.cloned.1.call-update
  9.5 0.0 reduce-scatter.5.cloned.1.call-start
  9.6 42.8 %all-gather.3.cloned.1.call-done = bf16[512,4096]{0,1:T(8,128)(2,1)} async-done(((bf16[512,1024]{0,1:T(8,128)(2,1)}), bf16[512,4096]{0,1:T(8,128)(2,1)}) %all-gather.3.cloned.1.call-update) | async-done | bytes 4194320 | tf_op jit(solution)/shard_map/all_gather | solution.py:49
  52.3 1.3 constant_dynamic-slice_fusion.1
  53.6 9.0 %multiply_convert_fusion.1 = bf16[1024,4096]{1,0:T(8,128)(2,1)} fusion(bf16[512,1024]{0,1:T(8,128)(2,1)S(1)} %bitcast.18, bf16[512,4096]{0,1:T(8,128)(2,1)} %all-gather.3.cloned.1.call-done), kind=kOutput, calls=%fused_computation.1 | convolution fusion | flops 4303355904 | bytes 13631488 | tf_op jit(solution)/shard_map/dot_general | solution.py:41
  62.6 7.7 %copy.8 = bf16[4,4,2,32,4096]{4,3,2,1,0:T(8,128)(2,1)} copy(bf16[4,4,2,32,4096]{4,3,1,0,2:T(8,128)(2,1)} %bitcast.16) | data formatting | bytes 16777216 | tf_op jit(solution)/shard_map/transpose | solution.py:14
  70.3 0.0 copy-start
  70.4 0.0 reduce-scatter.5.cloned.1.call-update
  70.4 0.0 all-gather.5.cloned.1.call-start
  70.4 1.4 copy-done
  71.8 2.3 copy.9
  74.1 0.0 all-gather.5.cloned.1.call-update
  74.2 0.0 reduce-scatter.7.cloned.1.call-start
  74.2 76.1 %reduce-scatter.5.cloned.1.call-done = bf16[8,32,4096]{2,1,0:T(8,128)(2,1)} async-done(((bf16[32,32,4096]{2,1,0:T(8,128)(2,1)}), bf16[8,32,4096]{2,1,0:T(8,128)(2,1)}) %reduce-scatter.5.cloned.1.call-update) | async-done | bytes 2097168 | tf_op jit(solution)/shard_map/reduce_scatter | solution.py:16
  150.3 0.0 reduce-scatter.7.cloned.1.call-update
  150.3 0.0 reduce-scatter.9.cloned.1.call-start
  150.3 58.0 %all-gather.5.cloned.1.call-done = bf16[512,7168]{0,1:T(8,128)(2,1)} async-done(((bf16[512,1792]{0,1:T(8,128)(2,1)}), bf16[512,7168]{0,1:T(8,128)(2,1)}) %all-gather.5.cloned.1.call-update) | async-done | bytes 7340048 | tf_op jit(solution)/shard_map/all_gather | solution.py:50
  208.4 1.6 constant_dynamic-slice_fusion
  210.0 29.3 %reduce-scatter.7.cloned.1.call-done = bf16[2,32,4096]{2,1,0:T(8,128)(2,1)} async-done(((bf16[8,32,4096]{2,1,0:T(8,128)(2,1)}), bf16[2,32,4096]{2,1,0:T(8,128)(2,1)}) %reduce-scatter.7.cloned.1.call-update) | async-done | bytes 524304 | tf_op jit(solution)/shard_map/reduce_scatter | solution.py:16
  239.3 0.0 reduce-scatter.9.cloned.1.call-update
  239.4 0.0 reduce-scatter.11.cloned.1.call-start
  239.4 20.0 %multiply_convert_fusion = bf16[1792,7168]{1,0:T(8,128)(2,1)} fusion(bf16[512,1792]{0,1:T(8,128)(2,1)S(1)} %bitcast.17, bf16[512,7168]{0,1:T(8,128)(2,1)} %all-gather.5.cloned.1.call-done), kind=kOutput, calls=%fused_computation | convolution fusion | flops 13179027456 | bytes 34865152 | tf_op jit(solution)/shard_map/dot_general | solution.py:41
  259.4 0.0 copy-start.2
  259.4 0.0 reduce-scatter.11.cloned.1.call-update
  259.4 0.0 reduce-scatter.9.cloned.1.call-done
  259.5 1.0 copy-done.2
  260.5 1.8 fusion
  262.3 282.4 %reduce-scatter.11.cloned.1.call-done = bf16[56,7168]{1,0:T(8,128)(2,1)} async-done(((bf16[1792,7168]{1,0:T(8,128)(2,1)}), bf16[56,7168]{1,0:T(8,128)(2,1)}) %reduce-scatter.11.cloned.1.call-update) | async-done | bytes 802832 | tf_op jit(solution)/shard_map/reduce_scatter | solution.py:71
  544.7 0.0 copy-done.1
  544.7 2.5 add_multiply_fusion
  (1 shorter events, 0.0 us)
Async XLA Ops:
  7.2 45.2 %all-gather.3.cloned.1.call-start = ((), (), s32[]{:S(2)}) async-start(), calls=%async_computation.4 | async-start | bytes 5242880 | tf_op jit(solution)/shard_map/all_gather | solution.py:49
  9.5 140.8 %reduce-scatter.5.cloned.1.call-start = ((), (), s32[]{:S(2)}) async-start(), calls=%async_computation.5 | async-start | bytes 10485760 | tf_op jit(solution)/shard_map/reduce_scatter | solution.py:16
  70.3 1.5 copy-start
  70.4 138.0 %all-gather.5.cloned.1.call-start = ((), (), s32[]{:S(2)}) async-start(), calls=%async_computation.8 | async-start | bytes 9175040 | tf_op jit(solution)/shard_map/all_gather | solution.py:50
  74.2 165.2 %reduce-scatter.7.cloned.1.call-start = ((), (), s32[]{:S(2)}) async-start(), calls=%async_computation.6 | async-start | bytes 2621440 | tf_op jit(solution)/shard_map/reduce_scatter | solution.py:16
  150.3 109.2 %reduce-scatter.9.cloned.1.call-start = ((), (), s32[]{:S(2)}) async-start(), calls=%async_computation.7 | async-start | bytes 786432 | tf_op jit(solution)/shard_map/reduce_scatter | solution.py:16
  239.4 305.3 %reduce-scatter.11.cloned.1.call-start = ((), (), s32[]{:S(2)}) async-start(), calls=%async_computation.9 | async-start | bytes 26492928 | tf_op jit(solution)/shard_map/reduce_scatter | solution.py:71
  259.4 1.0 copy-start.2
  259.4 285.3 %copy-start.1 = (f32[56,7168]{1,0:T(8,128)S(1)}, f32[56,7168]{1,0:T(8,128)}, u32[]{:S(2)}) copy-start(f32[56,7168]{1,0:T(8,128)} %param.7) | copy-start | bytes 4816900
Sparse Core Ops, SparseCore 0:
  10.2 42.0 all-gather.2
  70.5 79.7 reduce-scatter.4
  151.9 56.3 all-gather.4
  210.6 28.6 reduce-scatter.6
  241.5 16.7 reduce-scatter.8
  260.6 284.0 reduce-scatter.10
where the time goes:
time: 554 us
  waiting for transfers between devices  489 us (88%)
  matrix products  29 us (5%)
  local copies, waits for them, and re-layouts  17.6 us (3%)
  between operations  14.1 us (3%)
    reduce_scatter x1, waiting for transfers between devices, body(): lax.psum_scatter(full_term(full_grads, tensor_index, tensor_count, grad_w...  282 us
    reduce_scatter x3, waiting for transfers between devices, own_block(): blocks = lax.psum_scatter(blocks, axes[k], scatter_dimension=0, tiled=True)  105 us
    all_gather x1, waiting for transfers between devices, body(): lax.all_gather(gradients, ('tr', 'tc'), axis=1, tiled=True)  58 us
    all_gather x1, waiting for transfers between devices, body(): lax.all_gather(activations, ('tr', 'tc'), axis=1, tiled=True)  42.8 us
    dot_general x2, matrix products, full_term(): lax.dot_general(left_rows, gathered, (((0,), (0,)), ((), ())), preferred_...  29 us
  transfers between devices with their start and end apart: 6, of which 5 were waited for; matrix products, arithmetic and copies ran while one was open for 5% of the time, Pallas kernels for 0%

commit v1 on v0

v1 whole, which is shorter than its diff:
```python
import functools

import jax
import jax.numpy as jnp
from jax import lax
from jax.experimental import pallas as pl
from jax.experimental.pallas import tpu as pltpu
from jax.sharding import Mesh
from jax.sharding import PartitionSpec as P

MESH = pl.DeviceIdType.MESH
DP = ("dp_0", "dp_1", "dp_2")
DP_TR_TC = ("dp_0", "dp_1", "dp_2", "tr", "tc")
AXES = DP_TR_TC

ACT, GRAD = 0, 1
PIECES = (
    (ACT, 0, 512, 0),
    (ACT, 512, 512, 1),
    (GRAD, 0, 512, 0),
    (GRAD, 512, 384, 0),
    (GRAD, 896, 512, 1),
    (GRAD, 1408, 384, 1),
)


def pieces_of(m, half):
    return [i for i, p in enumerate(PIECES) if p[0] == m and p[3] == half]


def kernel(
    act, grad, out_a, out_g,
    buf_a, buf_g, prod_a, prod_g, recv_a, recv_g, fin_a, fin_g,
    own_sem, a_send, a_recv, b_send, b_recv, d_send, d_recv,
    s_send, s_recv, f_send, f_recv, o_sem,
):
    h = lax.axis_index("dp_0")
    z = lax.axis_index("dp_1")
    y = lax.axis_index("dp_2")
    tr = lax.axis_index("tr")
    tc = lax.axis_index("tc")
    is_n = (tr + h) % 2

    src = (act, grad)
    out = (out_a, out_g)
    buf = (buf_a, buf_g)
    prod = (prod_a, prod_g)
    recv = (recv_a, recv_g)
    fin = (fin_a, fin_g)

    def flip1(v):
        return v + 1 - 2 * (v % 2)

    def flip3(v):
        return 3 - v

    x1 = (1 - h, z, y, tr, tc)
    x3 = (1 - h, z, y, tr, 1 - tc)
    core = (h, z, y, 1 - tr, tc)
    others = ((h, z, y, tr, 1 - tc), core, (h, z, y, 1 - tr, 1 - tc))

    def partner(d):
        f = flip1 if d % 2 == 0 else flip3
        on_y = (1 - tr) if d < 2 else tr
        return (
            h,
            on_y * z + (1 - on_y) * f(z),
            on_y * f(y) + (1 - on_y) * y,
            tr,
            tc,
        )

    barrier = pltpu.get_barrier_semaphore()
    peers = [x1, x3, *others, *(partner(d) for d in range(4))]
    for peer in peers:
        pl.semaphore_signal(barrier, inc=1, device_id=peer, device_id_type=MESH)

    own = [pltpu.make_async_copy(src[m], buf[m].at[0], own_sem.at[m]) for m in (ACT, GRAD)]
    for copy in own:
        copy.start()
    pl.semaphore_wait(barrier, len(peers))

    def cols(i):
        return pl.ds(PIECES[i][1], PIECES[i][2])

    def remote(a, b, ss, rs, to):
        return pltpu.make_async_remote_copy(
            src_ref=a, dst_ref=b, send_sem=ss, recv_sem=rs, device_id=to, device_id_type=MESH
        )

    def along_a(i):
        m = PIECES[i][0]
        return remote(
            src[m].at[:, cols(i)], buf[m].at[1, :, cols(i)], a_send.at[i], a_recv.at[i], x1
        )

    def along_b(k, i):
        m = PIECES[i][0]
        source = src[m].at[:, cols(i)] if k == 0 else buf[m].at[1, :, cols(i)]
        return remote(
            source, buf[m].at[3 - k, :, cols(i)], b_send.at[k, i], b_recv.at[k, i], x3
        )

    def to_core(k, i):
        m = PIECES[i][0]
        source = src[m].at[:, cols(i)] if k == 0 else buf[m].at[k, :, cols(i)]
        slot = k + 4 if k < 2 else k
        return remote(
            source, buf[m].at[slot, :, cols(i)], d_send.at[k, i], d_recv.at[k, i], core
        )

    every = range(len(PIECES))
    for i in every:
        along_a(i).start()

    @pl.when(is_n == 1)
    def _():
        for i in every:
            along_b(0, i).start()

    @pl.when(is_n == 0)
    def _():
        for i in every:
            to_core(0, i).start()

    def step_a(m, half):
        for i in pieces_of(m, half):
            along_a(i).wait_recv()

            @pl.when(is_n == 1)
            def _(i=i):
                along_b(1, i).start()

            @pl.when(is_n == 0)
            def _(i=i):
                to_core(1, i).start()

        @pl.when(is_n == 1)
        def _():
            for i in pieces_of(m, half):
                to_core(0, i).wait_recv()
                to_core(1, i).wait_recv()

    def step_b(m, half):
        @pl.when(is_n == 0)
        def _():
            for i in pieces_of(m, half):
                along_b(0, i).wait_recv()
                to_core(3, i).start()
            for i in pieces_of(m, half):
                along_b(1, i).wait_recv()
                to_core(2, i).start()

        @pl.when(is_n == 1)
        def _():
            for i in pieces_of(m, half):
                to_core(3, i).wait_recv()
                to_core(2, i).wait_recv()

    zb = z // 2
    za = (z + zb) % 2
    yb = y // 2
    ya = (y + yb) % 2

    def weight(d0, d1, s):
        w = [[2 ** ((d - k) % 4) for k in (0, 1)] for d in (d0, d1)]
        on0 = w[0][0] + s * (w[0][1] - w[0][0])
        on1 = w[1][0] + s * (w[1][1] - w[1][0])
        return on0 + tr * (on1 - on0)

    def first_partner(s):
        def f(v):
            return (1 - s) * flip1(v) + s * flip3(v)

        return (h, (1 - tr) * z + tr * f(z), (1 - tr) * f(y) + tr * y, tr, tc)

    def stream_copy(m, s, q, to):
        return remote(
            prod[m].at[s, q], recv[m].at[s, q], s_send.at[m, s, q], s_recv.at[m, s, q], to
        )

    def product(m, e, c, s):
        half = buf[m].shape[2] // 2
        rows = half // 4
        tokens = 2 * buf[m].shape[1]
        base = e * 2 + (1 - e) * 4 * is_n
        left = buf[m][pl.ds(base, 2), :, pl.ds(pl.multiple_of(c * half, 128), half)]
        right = buf[m][pl.ds(0, 2), :, pl.ds(pl.multiple_of(s * half, 128), half)]
        value = lax.dot_general(
            left.reshape(tokens, half),
            right.reshape(tokens, half),
            (((0,), (0,)), ((), ())),
            preferred_element_type=jnp.float32,
        )
        block = (tc + e) % 2
        rza = (c + block + za) % 2
        rzb = (block + zb) % 2
        zq = rza * weight(2, 0, s) + rzb * weight(3, 1, s)
        for yy in range(4):
            rya = ((yy ^ (yy >> 1)) % 2 + ya) % 2
            ryb = (yy // 2 + yb) % 2
            q = zq + rya * weight(0, 2, s) + ryb * weight(1, 3, s)
            prod[m][s, q] = value[yy * rows : (yy + 1) * rows].astype(jnp.bfloat16)

            @pl.when(q % 2 == 1)
            def _(q=q):
                stream_copy(m, s, q, first_partner(s)).start()

    def arrived(m, s, q):
        stream_copy(m, s, q, core).wait_recv()

    def total(m, s, q, parts):
        value = prod[m][s, q].astype(jnp.float32)
        for p in parts:
            value = value + recv[m][s, p].astype(jnp.float32)
        return value

    def stage(m, s, k):
        to = partner((k + s) % 4)

        def one(i, carry):
            q = i * 2 ** (k + 1) + 2**k
            parts = [q + 2**j for j in range(k)]
            for p in parts:
                arrived(m, s, p)
            prod[m][s, q] = total(m, s, q, parts).astype(jnp.bfloat16)
            stream_copy(m, s, q, to).start()
            return carry

        lax.fori_loop(0, 2 ** (3 - k), one, 0)

    def place(m, s):
        width = buf[m].shape[2]
        half = width // 2
        first = pl.multiple_of((2 * tr + tc) * width + s * half, 128)
        return out[m].at[:, pl.ds(first, half)]

    def last_copy(m, s, k):
        half = buf[m].shape[2] // 2
        to = others[k]
        return remote(
            fin[m].at[2 * to[3] + to[4], :, pl.ds(s * half, half)],
            place(m, s),
            f_send.at[m, s, k],
            f_recv.at[m, s, k],
            to,
        )

    def own_copy(m, s):
        half = buf[m].shape[2] // 2
        return pltpu.make_async_copy(
            fin[m].at[2 * tr + tc, :, pl.ds(s * half, half)], place(m, s), o_sem.at[m, s]
        )

    def finish(m, s):
        parts = [1, 2, 4, 8]
        for p in parts:
            arrived(m, s, p)
        half = buf[m].shape[2] // 2
        rows = half // 16
        value = total(m, s, 0, parts)
        for k in range(4):
            fin[m][k, :, pl.ds(s * half, half)] = value[k * rows : (k + 1) * rows].astype(
                jnp.bfloat16
            )
        for k in range(3):
            last_copy(m, s, k).start()
        own_copy(m, s).start()

    def loop(m, first, last, which):
        def one(j, carry):
            product(m, *which(j))
            return carry

        lax.fori_loop(first, last, one, 0)

    for copy in own:
        copy.wait()

    def products_a(m):
        step_a(m, 0)
        step_a(m, 1)
        loop(m, 0, 4, lambda j: (0, j % 2, j // 2))

    def products_b(m):
        step_b(m, 0)
        step_b(m, 1)
        loop(m, 0, 4, lambda j: (1, j // 2, j % 2))

    products_a(ACT)
    products_b(ACT)
    step_a(GRAD, 0)
    for k in (1, 2):
        for s in (0, 1):
            stage(ACT, s, k)
    step_a(GRAD, 1)
    loop(GRAD, 0, 4, lambda j: (0, j % 2, j // 2))
    for s in (0, 1):
        stage(ACT, s, 3)
    for s in (0, 1):
        finish(ACT, s)
    products_b(GRAD)
    for k in (1, 2, 3):
        for s in (0, 1):
            stage(GRAD, s, k)
    for s in (0, 1):
        finish(GRAD, s)

    for i in every:
        along_a(i).wait_send()

    @pl.when(is_n == 1)
    def _():
        for i in every:
            for k in (0, 1):
                along_b(k, i).wait_send()

    @pl.when(is_n == 0)
    def _():
        for i in every:
            for k in range(4):
                to_core(k, i).wait_send()

    for m in (ACT, GRAD):
        for s in (0, 1):
            for q in range(1, 16):
                stream_copy(m, s, q, core).wait_send()
            own_copy(m, s).wait()
            for k in range(3):
                last_copy(m, s, k).wait()


def sums(activations, gradients, rows_a, rows_g):
    tokens = activations.shape[0]
    wide = (activations.shape[1], gradients.shape[1])
    rows = (rows_a, rows_g)
    bf16 = jnp.bfloat16
    vmem = [
        *(pltpu.VMEM((6, tokens, w), bf16) for w in wide),
        *(pltpu.VMEM((2, 16, w // 8, w // 2), bf16) for w in wide),
        *(pltpu.VMEM((2, 16, w // 8, w // 2), bf16) for w in wide),
        *(pltpu.VMEM((4, r, w), bf16) for r, w in zip(rows, wide)),
    ]
    n = len(PIECES)
    dma = pltpu.SemaphoreType.DMA
    sems = [
        dma((2,)), dma((n,)), dma((n,)), dma((2, n)), dma((2, n)), dma((4, n)), dma((4, n)),
        dma((2, 2, 16)), dma((2, 2, 16)), dma((2, 2, 3)), dma((2, 2, 3)), dma((2, 2)),
    ]
    anywhere = pl.BlockSpec(memory_space=pl.ANY)
    return pl.pallas_call(
        kernel,
        out_shape=[jax.ShapeDtypeStruct((r, 4 * w), bf16) for r, w in zip(rows, wide)],
        in_specs=[anywhere] * 2,
        out_specs=[anywhere] * 2,
        scratch_shapes=[*vmem, *sems],
        compiler_params=pltpu.CompilerParams(
            collective_id=0, has_side_effects=True, vmem_limit_bytes=66_000_000
        ),
    )(activations, gradients)


def body(activations, gradients, old_inputs, old_gradients):
    tokens_all = activations.shape[0] * lax.axis_size(DP)
    sum_a, sum_g = sums(activations, gradients, old_inputs.shape[0], old_gradients.shape[0])
    scale = 0.5 / tokens_all
    return (
        0.5 * old_inputs + scale * sum_a.astype(jnp.float32),
        0.5 * old_gradients + scale * sum_g.astype(jnp.float32),
    )


def solution(mesh):
    finer = Mesh(mesh.devices.reshape(2, 4, 4, mesh.shape["tr"], mesh.shape["tc"]), AXES)
    return jax.shard_map(
        body,
        mesh=finer,
        in_specs=(P(DP, ("tr", "tc")), P(DP, ("tr", "tc")), P(DP_TR_TC, None), P(DP_TR_TC, None)),
        out_specs=(P(DP_TR_TC, None), P(DP_TR_TC, None)),
        check_vma=False,
    )
```

time: 554 us -> 201 us (0.36)
  waiting for transfers between devices: 489 us -> 0 us
  Pallas kernels: 0 us -> 196 us
  matrix products: 29 us -> 0 us
  local copies, waits for them, and re-layouts: 17.6 us -> 0.01 us
  between operations: 14.1 us -> 0.65 us
    reduce_scatter x4 -> x0, waiting for transfers between devices: 388 us -> none  [the longest x1 282 us: body(): lax.psum_scatter(full_term(full_grads, tensor_index, tensor_count, grad_w...]
    pallas_call x0 -> x1, Pallas kernels: none -> 196 us  [sums(): pl.pallas_call(kernel, out_shape=[jax.ShapeDtypeStruct((r, 4 * w), bf16)...]
    all_gather x2 -> x0, waiting for transfers between devices: 101 us -> none  [the longest x1 58 us: body(): lax.all_gather(gradients, ('tr', 'tc'), axis=1, tiled=True)]
    dot_general x2 -> x0, matrix products: 29 us -> none  [full_term(): lax.dot_general(left_rows, gathered, (((0,), (0,)), ((), ())), preferred_...]
    transpose x1 -> x0, local copies, waits for them, and re-layouts: 7.72 us -> none  [own_block(): jnp.moveaxis(blocks, sequence, range(len(axes))).reshape(-1, *inside)]
    unnamed x8 -> x4, local copies, waits for them, and re-layouts: 6.98 us -> 0.01 us
  transfers between devices with their start and end apart: 6 -> 0, of which waited for: 5 -> 0; matrix products, arithmetic and copies ran while one was open for 5% -> 0% of each run, Pallas kernels for 0% -> 0%
where the time goes in v1:
time: 201 us; the launch traced here: 200 us
  Pallas kernels  196 us (98%)
  other arithmetic  3.96 us (2%)
    pallas_call x1, Pallas kernels, sums(): pl.pallas_call(kernel, out_shape=[jax.ShapeDtypeStruct((r, 4 * w), bf16)...  196 us

profile of v1, /device:TPU:1, one launch (start us, length us, event | category | flops | bytes accessed | tf_op | source)
XLA Modules:
  0.0 200.3 jit_solution(4582118733206328374)
XLA Ops:
  0.6 195.7 %shard_map.59 = (bf16[32,4096]{1,0:T(8,128)(2,1)}, bf16[56,7168]{1,0:T(8,128)(2,1)}) custom-call(bf16[512,1024]{1,0:T(8,128)(2,1)} %act.1, bf16[512,1792]{1,0:T(8,128)(2,1)} %grad.1), custom_call_target="tpu_custom_call" | custom-call | tf_op jit(solution)/shard_map/pallas_call | solution.py:351
  196.3 0.0 copy-start
  196.3 0.0 copy-start.1
  196.3 3.1 %multiply_add_fusion = f32[56,7168]{1,0:T(8,128)} fusion(bf16[56,7168]{1,0:T(8,128)(2,1)} %get-tuple-element.5, f32[56,7168]{1,0:T(8,128)} %param.7), kind=kLoop, calls=%fused_computation | loop fusion | flops 1605632 | bytes 4014080 | tf_op jit(solution)/shard_map/add | solution.py:369
  199.4 0.0 copy-done
  199.4 0.0 copy-done.1
  199.4 0.9 multiply_add_fusion.1
Async XLA Ops:
  196.3 3.1 %copy-start = (f32[32,4096]{1,0:T(8,128)S(1)}, f32[32,4096]{1,0:T(8,128)}, u32[]{:S(2)}) copy-start(f32[32,4096]{1,0:T(8,128)} %param.6) | copy-start | bytes 1572868
  196.3 3.1 %copy-start.1 = (bf16[32,4096]{1,0:T(8,128)(2,1)S(1)}, bf16[32,4096]{1,0:T(8,128)(2,1)}, u32[]{:S(2)}) copy-start(bf16[32,4096]{1,0:T(8,128)(2,1)} %get-tuple-element.4) | copy-start | bytes 786436

commit v2 on v1

v2 whole, which is shorter than its diff:
```python
import functools

import jax
import jax.numpy as jnp
from jax import lax
from jax.experimental import pallas as pl
from jax.experimental.pallas import tpu as pltpu
from jax.sharding import Mesh
from jax.sharding import PartitionSpec as P

MESH = pl.DeviceIdType.MESH
DP = ("dp_0", "dp_1", "dp_2")
DP_TR_TC = ("dp_0", "dp_1", "dp_2", "tr", "tc")
AXES = DP_TR_TC

ACT, GRAD = 0, 1
PIECES = (
    (GRAD, 0, 512, 0),
    (GRAD, 512, 384, 0),
    (GRAD, 896, 512, 1),
    (GRAD, 1408, 384, 1),
    (ACT, 0, 512, 0),
    (ACT, 512, 512, 1),
)
EARLY = 3


def pieces_of(m, half):
    return [i for i, p in enumerate(PIECES) if p[0] == m and p[3] == half]


def scoped(name, f):
    def g(*a):
        with jax.named_scope(name + "#" + "_".join(str(x) for x in a if isinstance(x, int))):
            return f(*a)

    return g


def kernel(
    act, grad, out_a, out_g,
    buf_a, buf_g, prod_a, prod_g, recv_a, recv_g, prox_a, prox_g, recx_a, recx_g,
    fin_a, fin_g, finx_a, finx_g, turn_a, turn_g, mir_a, mir_g, row_a, row_g,
    own_sem, a_send, a_recv, b_send, b_recv, d_send, d_recv,
    s_send, s_recv, x_send, x_recv, f_send, f_recv, g_send, g_recv, m_send, m_recv, o_sem,
):
    h = lax.axis_index("dp_0")
    z = lax.axis_index("dp_1")
    y = lax.axis_index("dp_2")
    tr = lax.axis_index("tr")
    tc = lax.axis_index("tc")
    is_n = (tr + h) % 2

    src = (act, grad)
    out = (out_a, out_g)
    buf = (buf_a, buf_g)
    prod = (prod_a, prod_g)
    recv = (recv_a, recv_g)
    prox = (prox_a, prox_g)
    recx = (recx_a, recx_g)
    fin = (fin_a, fin_g)
    finx = (finx_a, finx_g)
    turn = (turn_a, turn_g)
    mir = (mir_a, mir_g)
    row = (row_a, row_g)

    def flip1(v):
        return v + 1 - 2 * (v % 2)

    def flip3(v):
        return 3 - v

    x1 = (1 - h, z, y, tr, tc)
    x3 = (1 - h, z, y, tr, 1 - tc)
    core = (h, z, y, 1 - tr, tc)
    others = ((h, z, y, tr, 1 - tc), core, (h, z, y, 1 - tr, 1 - tc))
    y_a, y_b = (h, z, flip1(y), tr, tc), (h, z, flip3(y), tr, tc)
    z_a, z_b = (h, flip1(z), y, tr, tc), (h, flip3(z), y, tr, tc)

    def partner(d):
        f = flip1 if d % 2 == 0 else flip3
        on_y = (1 - tr) if d < 2 else tr
        return (
            h,
            on_y * z + (1 - on_y) * f(z),
            on_y * f(y) + (1 - on_y) * y,
            tr,
            tc,
        )

    half_z = z // 2
    c_mine = z % 2
    apart = (half_z + tc) % 2
    side = (c_mine + apart * tc + (1 - apart) * is_n * h) % 2
    mirrors = 1 - (1 - is_n) * (1 - apart)
    kind = is_n * (1 + apart)
    turned_rows = (
        4 * h + 2 * (1 - half_z) + (c_mine + half_z) % 2,
        4 * (1 - h) + 2 * half_z + (c_mine + 1 - h) % 2,
        4 * (1 - h) + 2 * (1 - half_z) + (c_mine + half_z) % 2,
    )

    def quarters():
        for yy in range(4):
            for aa in range(2):
                for bb in range(2):
                    yield yy * 4 + aa * 2 + bb, (tr, 2 * tc + side, yy, aa, bb)

    barrier = pltpu.get_barrier_semaphore()
    peers = [x1, x3, *others, y_a, y_b, z_a, z_b]

    def greet(peer):
        pl.semaphore_signal(barrier, inc=1, device_id=peer, device_id_type=MESH)

    for peer in peers:
        greet(peer)
    for chunk in turned_rows:
        for yy in range(4):
            greet((chunk // 4, chunk % 4, yy, h, half_z))

    own = [pltpu.make_async_copy(src[m], buf[m].at[0], own_sem.at[m]) for m in (ACT, GRAD)]
    for copy in own:
        copy.start()
    pl.semaphore_wait(barrier, len(peers) + 16 * mirrors)

    def cols(i):
        return pl.ds(PIECES[i][1], PIECES[i][2])

    def remote(a, b, ss, rs, to):
        return pltpu.make_async_remote_copy(
            src_ref=a, dst_ref=b, send_sem=ss, recv_sem=rs, device_id=to, device_id_type=MESH
        )

    def along_a(i):
        m = PIECES[i][0]
        return remote(
            src[m].at[:, cols(i)], buf[m].at[1, :, cols(i)], a_send.at[i], a_recv.at[i], x1
        )

    def along_b(k, i):
        m = PIECES[i][0]
        source = src[m].at[:, cols(i)] if k == 0 else buf[m].at[1, :, cols(i)]
        return remote(
            source, buf[m].at[3 - k, :, cols(i)], b_send.at[k, i], b_recv.at[k, i], x3
        )

    def to_core(k, i):
        m = PIECES[i][0]
        source = src[m].at[:, cols(i)] if k == 0 else buf[m].at[k, :, cols(i)]
        slot = k + 4 if k < 2 else k
        return remote(
            source, buf[m].at[slot, :, cols(i)], d_send.at[k, i], d_recv.at[k, i], core
        )

    every = range(len(PIECES))
    for i in every:
        along_a(i).start()

    @pl.when(is_n == 1)
    def _():
        for i in range(EARLY):
            along_b(0, i).start()

    @pl.when(is_n == 0)
    def _():
        for i in every:
            to_core(0, i).start()

    def step_a(m, half):
        for i in pieces_of(m, half):
            along_a(i).wait_recv()

            @pl.when(is_n == 1)
            def _(i=i):
                along_b(1, i).start()
                if 1 <= i and i + EARLY - 1 in every:
                    along_b(0, i + EARLY - 1).start()

            @pl.when(is_n == 0)
            def _(i=i):
                to_core(1, i).start()

        @pl.when(is_n == 1)
        def _():
            for i in pieces_of(m, half):
                to_core(0, i).wait_recv()
                to_core(1, i).wait_recv()

    def step_b(m, half):
        @pl.when(is_n == 0)
        def _():
            for i in pieces_of(m, half):
                along_b(0, i).wait_recv()
                to_core(3, i).start()
            for i in pieces_of(m, half):
                along_b(1, i).wait_recv()
                to_core(2, i).start()

        @pl.when(is_n == 1)
        def _():
            for i in pieces_of(m, half):
                to_core(3, i).wait_recv()
                to_core(2, i).wait_recv()

    zb = z // 2
    za = (z + zb) % 2
    yb = y // 2
    ya = (y + yb) % 2

    def weight(d0, d1, k):
        on0, on1 = 2 ** ((d0 - k) % 4), 2 ** ((d1 - k) % 4)
        return on0 + tr * (on1 - on0)

    def stream_copy(m, k, q, to):
        return remote(
            prod[m].at[k, q], recv[m].at[k, q], s_send.at[m, k, q], s_recv.at[m, k, q], to
        )

    def extra_copy(m, k, q, to):
        return remote(
            prox[m].at[k, q], recx[m].at[k, q], x_send.at[m, k, q], x_recv.at[m, k, q], to
        )

    def dot(m, e, c, s):
        half = buf[m].shape[2] // 2
        tokens = 2 * buf[m].shape[1]
        base = e * 2 + (1 - e) * 4 * is_n
        left = buf[m][pl.ds(base, 2), :, pl.ds(pl.multiple_of(c * half, 128), half)]
        right = buf[m][pl.ds(0, 2), :, pl.ds(pl.multiple_of(s * half, 128), half)]
        return lax.dot_general(
            left.reshape(tokens, half),
            right.reshape(tokens, half),
            (((0,), (0,)), ((), ())),
            preferred_element_type=jnp.float32,
        )

    def bits_of(yy):
        return ((yy ^ (yy >> 1)) % 2 + ya) % 2, (yy // 2 + yb) % 2

    def product(m, e, c):
        value = dot(m, e, c, (c + (e * tc if e else is_n * h)) % 2)
        rows = value.shape[0] // 8
        block = (tc + e) % 2
        rza = (c + block + za) % 2
        rzb = (block + zb) % 2
        for yy in range(4):
            rya, ryb = bits_of(yy)
            for k in range(2):
                q = rza * weight(2, 0, k) + rzb * weight(3, 1, k)
                q = q + rya * weight(0, 2, k) + ryb * weight(1, 3, k)
                first = (2 * yy + k) * rows
                prod[m][k, q] = value[first : first + rows].astype(jnp.bfloat16)

                @pl.when(q % 2 == 1)
                def _(k=k, q=q):
                    stream_copy(m, k, q, partner(k)).start()

    EXTRA = ((y_a, y_b, z_a), (z_a, y_b, y_a))

    def product_extra(m, c):
        value = dot(m, 0, c, 1 - c)
        rows = value.shape[0] // 8
        rza = (c + tc + za) % 2
        for yy in range(4):
            rya, ryb = bits_of(yy)
            for k in range(2):
                q = rya + 2 * ryb + 4 * rza if k == 0 else rza + 2 * ryb + 4 * rya
                first = (2 * yy + k) * rows
                prox[m][k, q] = value[first : first + rows].astype(jnp.bfloat16)

                @pl.when(q % 2 == 1)
                def _(k=k, q=q):
                    extra_copy(m, k, q, EXTRA[k][0]).start()

    def total(own_ref, got_ref, k, q, parts):
        value = own_ref[k, q].astype(jnp.float32)
        for p in parts:
            value = value + got_ref[k, p].astype(jnp.float32)
        return value

    def stage(m, j):
        for k in range(2):
            to = partner((j + k) % 4)

            def one(i, carry, k=k, to=to):
                q = i * 2 ** (j + 1) + 2**j
                parts = [q + 2**b for b in range(j)]
                for p in parts:
                    stream_copy(m, k, p, core).wait_recv()
                prod[m][k, q] = total(prod[m], recv[m], k, q, parts).astype(jnp.bfloat16)
                stream_copy(m, k, q, to).start()
                return carry

            lax.fori_loop(0, 2 ** (3 - j), one, 0)

    def stage_extra(m, j):
        @pl.when(is_n == 0)
        def _():
            for k in range(2):
                if j < 3:

                    def one(i, carry, k=k):
                        q = i * 2 ** (j + 1) + 2**j
                        parts = [q + 2**b for b in range(j)]
                        for p in parts:
                            extra_copy(m, k, p, core).wait_recv()
                        prox[m][k, q] = total(prox[m], recx[m], k, q, parts).astype(
                            jnp.bfloat16
                        )
                        extra_copy(m, k, q, EXTRA[k][j]).start()
                        return carry

                    lax.fori_loop(0, 2 ** (2 - j), one, 0)
                else:
                    for p in (1, 2, 4):
                        extra_copy(m, k, p, core).wait_recv()

                    @pl.when(apart == 1)
                    def _(k=k):
                        prox[m][k, 0] = total(prox[m], recx[m], k, 0, (1, 2, 4)).astype(
                            jnp.bfloat16
                        )
                        extra_copy(m, k, 0, z_b).start()

    def at(m, block, s):
        width = buf[m].shape[2]
        half = width // 2
        first = pl.multiple_of(block * width + s * half, 128)
        return pl.ds(first, half)

    def last_copy(m, k):
        to = others[k]
        return remote(
            fin[m].at[2 * to[3] + to[4]],
            row[m].at[:, at(m, 2 * tr + tc, side)],
            f_send.at[m, k],
            f_recv.at[m, k],
            to,
        )

    def last_extra(m, k):
        to = others[k]
        return remote(
            finx[m].at[2 * to[3] + to[4]],
            row[m].at[:, at(m, 2 * tr + tc, 1 - c_mine)],
            g_send.at[m, k],
            g_recv.at[m],
            to,
        )

    def turned_copy(m, i, to):
        return remote(
            turn[m].at[i], mir[m].at[kind, y], m_send.at[m, i], m_recv.at[m, kind, y], to
        )

    def by_quarter(m, ref, value, s):
        rows = value.shape[0] // 4
        for i in range(4):
            ref[m][i] = value[i * rows : (i + 1) * rows].astype(jnp.bfloat16)
        row[m][:, at(m, 2 * tr + tc, s)] = ref[m][2 * tr + tc]

    def finish(m):
        parts = (1, 2, 4, 8)
        for k in range(2):
            for p in parts:
                stream_copy(m, k, p, core).wait_recv()
        value = jnp.concatenate(
            [total(prod[m], recv[m], k, 0, parts) for k in range(2)], axis=0
        )
        by_quarter(m, fin, value, side)
        for k in range(3):
            last_copy(m, k).start()

        @pl.when(mirrors == 1)
        def _():
            lanes = turn[m].shape[2]
            tall = value
            if lanes != value.shape[0]:
                fill = jnp.zeros((lanes - value.shape[0], value.shape[1]), jnp.float32)
                tall = jnp.concatenate([value, fill], axis=0)
            turned = tall.T
            rows = turned.shape[0] // 16
            for i, to in quarters():
                turn[m][i] = turned[i * rows : (i + 1) * rows].astype(jnp.bfloat16)
                turned_copy(m, i, to).start()

    def finish_extra(m):
        @pl.when(mirrors == 0)
        def _():
            for k in range(2):
                extra_copy(m, k, 0, core).wait_recv()
            value = jnp.concatenate(
                [total(prox[m], recx[m], k, 0, (1, 2, 4, 0)) for k in range(2)], axis=0
            )
            by_quarter(m, finx, value, 1 - c_mine)
            for k in range(3):
                last_extra(m, k).start()

    def gather_rows(m):
        width = buf[m].shape[2]
        rows = width // 8
        for t in range(3):
            for yy in range(4):
                remote(
                    turn[m].at[0], mir[m].at[t, yy], m_send.at[m, 0], m_recv.at[m, t, yy], core
                ).wait_recv()
            value = jnp.concatenate(
                [mir[m][t, yy].astype(jnp.float32)[:, :rows] for yy in range(4)], axis=1
            )
            chunk = turned_rows[t]
            row[m][:, at(m, chunk // 2, chunk % 2)] = value.astype(jnp.bfloat16)
        for k in range(3):
            last_copy(m, k).wait_recv()

        @pl.when(mirrors == 1)
        def _():
            last_extra(m, 0).wait_recv()

        own_out(m).start()

    def own_out(m):
        return pltpu.make_async_copy(row[m], out[m], o_sem.at[m])

    def products(m, e, first, last):
        def one(c, carry):
            product(m, e, c)
            return carry

        lax.fori_loop(first, last, one, 0)

    def extras(m):
        @pl.when(is_n == 0)
        def _():
            def one(c, carry):
                product_extra(m, c)
                return carry

            lax.fori_loop(0, 2, one, 0)

    step_a = scoped("step_a", step_a)
    step_b = scoped("step_b", step_b)
    products = scoped("products", products)
    extras = scoped("extras", extras)
    stage = scoped("stage", stage)
    stage_extra = scoped("stage_extra", stage_extra)
    finish = scoped("finish", finish)
    finish_extra = scoped("finish_extra", finish_extra)
    gather_rows = scoped("gather_rows", gather_rows)

    early_0 = 1 - is_n * h
    early_1 = 1 - tc

    for copy in own:
        copy.wait()
    step_a(GRAD, 0)
    products(GRAD, 0, 0, early_0)
    step_b(GRAD, 0)
    products(GRAD, 1, 0, early_1)
    step_a(GRAD, 1)
    products(GRAD, 0, early_0, 2)
    products(GRAD, 1, early_1, 1)
    extras(GRAD)
    step_b(GRAD, 1)
    products(GRAD, 1, 1, 2)
    step_a(ACT, 0)
    stage(GRAD, 1)
    stage_extra(GRAD, 1)
    step_a(ACT, 1)
    products(ACT, 0, 0, 2)
    extras(ACT)
    stage(GRAD, 2)
    stage_extra(GRAD, 2)
    step_b(ACT, 0)
    step_b(ACT, 1)
    products(ACT, 1, 0, 2)
    stage(GRAD, 3)
    stage_extra(GRAD, 3)
    stage(ACT, 1)
    stage_extra(ACT, 1)
    finish(GRAD)
    stage(ACT, 2)
    stage_extra(ACT, 2)
    finish_extra(GRAD)
    stage(ACT, 3)
    stage_extra(ACT, 3)
    finish(ACT)
    finish_extra(ACT)
    gather_rows(GRAD)
    gather_rows(ACT)

    with jax.named_scope("drain"):
        for i in every:
            along_a(i).wait_send()

        @pl.when(is_n == 1)
        def _():
            for i in every:
                for k in (0, 1):
                    along_b(k, i).wait_send()

        @pl.when(is_n == 0)
        def _():
            for i in every:
                for k in range(4):
                    to_core(k, i).wait_send()
            for m in (ACT, GRAD):
                for k in range(2):
                    for q in range(1, 8):
                        extra_copy(m, k, q, core).wait_send()

                    @pl.when(apart == 1)
                    def _(m=m, k=k):
                        extra_copy(m, k, 0, core).wait_send()

        for m in (ACT, GRAD):
            for k in range(2):
                for q in range(1, 16):
                    stream_copy(m, k, q, core).wait_send()
            for k in range(3):
                last_copy(m, k).wait_send()

            @pl.when(mirrors == 1)
            def _(m=m):
                for i, to in quarters():
                    turned_copy(m, i, to).wait_send()

            @pl.when(mirrors == 0)
            def _(m=m):
                for k in range(3):
                    last_extra(m, k).wait_send()

            own_out(m).wait()


def sums(activations, gradients, rows_a, rows_g):
    tokens = activations.shape[0]
    wide = (activations.shape[1], gradients.shape[1])
    rows = (rows_a, rows_g)
    bf16 = jnp.bfloat16
    lanes = [-(-w // 1024) * 128 for w in wide]
    vmem = [
        *(pltpu.VMEM((6, tokens, w), bf16) for w in wide),
        *(pltpu.VMEM((2, 16, w // 16, w // 2), bf16) for w in wide),
        *(pltpu.VMEM((2, 16, w // 16, w // 2), bf16) for w in wide),
        *(pltpu.VMEM((2, 8, w // 16, w // 2), bf16) for w in wide),
        *(pltpu.VMEM((2, 8, w // 16, w // 2), bf16) for w in wide),
        *(pltpu.VMEM((4, r, w // 2), bf16) for r, w in zip(rows, wide)),
        *(pltpu.VMEM((4, r, w // 2), bf16) for r, w in zip(rows, wide)),
        *(pltpu.VMEM((16, r, n), bf16) for r, n in zip(rows, lanes)),
        *(pltpu.VMEM((3, 4, r, n), bf16) for r, n in zip(rows, lanes)),
        *(pltpu.VMEM((r, 4 * w), bf16) for r, w in zip(rows, wide)),
    ]
    n = len(PIECES)
    dma = pltpu.SemaphoreType.DMA
    sems = [
        dma((2,)), dma((n,)), dma((n,)), dma((2, n)), dma((2, n)), dma((4, n)), dma((4, n)),
        dma((2, 2, 16)), dma((2, 2, 16)), dma((2, 2, 8)), dma((2, 2, 8)),
        dma((2, 3)), dma((2, 3)), dma((2, 3)), dma((2,)),
        dma((2, 16)), dma((2, 3, 4)), dma((2,)),
    ]
    anywhere = pl.BlockSpec(memory_space=pl.ANY)
    return pl.pallas_call(
        kernel,
        out_shape=[jax.ShapeDtypeStruct((r, 4 * w), bf16) for r, w in zip(rows, wide)],
        in_specs=[anywhere] * 2,
        out_specs=[anywhere] * 2,
        scratch_shapes=[*vmem, *sems],
        compiler_params=pltpu.CompilerParams(
            collective_id=0, has_side_effects=True, vmem_limit_bytes=66_000_000
        ),
    )(activations, gradients)


def body(activations, gradients, old_inputs, old_gradients):
    tokens_all = activations.shape[0] * lax.axis_size(DP)
    sum_a, sum_g = sums(activations, gradients, old_inputs.shape[0], old_gradients.shape[0])
    scale = 0.5 / tokens_all
    return (
        0.5 * old_inputs + scale * sum_a.astype(jnp.float32),
        0.5 * old_gradients + scale * sum_g.astype(jnp.float32),
    )


def solution(mesh):
    finer = Mesh(mesh.devices.reshape(2, 4, 4, mesh.shape["tr"], mesh.shape["tc"]), AXES)
    return jax.shard_map(
        body,
        mesh=finer,
        in_specs=(P(DP, ("tr", "tc")), P(DP, ("tr", "tc")), P(DP_TR_TC, None), P(DP_TR_TC, None)),
        out_specs=(P(DP_TR_TC, None), P(DP_TR_TC, None)),
        check_vma=False,
    )
```

time: 201 us -> 147 us (0.73)
  Pallas kernels: 196 us -> 142 us
    pallas_call x1, Pallas kernels: 196 us -> 142 us  [sums(): pl.pallas_call(kernel, out_shape=[jax.ShapeDtypeStruct((r, 4 * w), bf16)...]
where the time goes in v2:
time: 147 us
  Pallas kernels  142 us (97%)
  other arithmetic  3.96 us (3%)
    pallas_call x1, Pallas kernels, sums(): pl.pallas_call(kernel, out_shape=[jax.ShapeDtypeStruct((r, 4 * w), bf16)...  142 us
    add x1, other arithmetic, body(): 0.5 * old_gradients + scale * sum_g.astype(jnp.float32)  3.09 us

profile of v2, /device:TPU:1, one launch (start us, length us, event | category | flops | bytes accessed | tf_op | source)
XLA Modules:
  0.0 146.9 jit_solution(2233988717504909492)
XLA Ops:
  0.6 142.3 %shard_map.59 = (bf16[32,4096]{1,0:T(8,128)(2,1)}, bf16[56,7168]{1,0:T(8,128)(2,1)}) custom-call(bf16[512,1024]{1,0:T(8,128)(2,1)} %act.1, bf16[512,1792]{1,0:T(8,128)(2,1)} %grad.1), custom_call_target="tpu_custom_call" | custom-call | tf_op jit(solution)/shard_map/pallas_call | solution.py:562
  142.9 0.0 copy-start
  142.9 0.0 copy-start.1
  142.9 3.1 %multiply_add_fusion = f32[56,7168]{1,0:T(8,128)} fusion(bf16[56,7168]{1,0:T(8,128)(2,1)} %get-tuple-element.5, f32[56,7168]{1,0:T(8,128)} %param.7), kind=kLoop, calls=%fused_computation | loop fusion | flops 1605632 | bytes 4014080 | tf_op jit(solution)/shard_map/add | solution.py:580
  146.0 0.0 copy-done
  146.0 0.0 copy-done.1
  146.0 0.9 multiply_add_fusion.1
Async XLA Ops:
  142.9 3.1 %copy-start = (f32[32,4096]{1,0:T(8,128)S(1)}, f32[32,4096]{1,0:T(8,128)}, u32[]{:S(2)}) copy-start(f32[32,4096]{1,0:T(8,128)} %param.6) | copy-start | bytes 1572868
  142.9 3.1 %copy-start.1 = (bf16[32,4096]{1,0:T(8,128)(2,1)S(1)}, bf16[32,4096]{1,0:T(8,128)(2,1)}, u32[]{:S(2)}) copy-start(bf16[32,4096]{1,0:T(8,128)(2,1)} %get-tuple-element.4) | copy-start | bytes 786436

commit v3 on v2

--- a/solution.py
+++ b/solution.py
@@ -17,12 +17,13 @@
 PIECES = (
     (GRAD, 0, 512, 0),
     (GRAD, 512, 384, 0),
-    (GRAD, 896, 512, 1),
-    (GRAD, 1408, 384, 1),
+    (GRAD, 0, 512, 1),
+    (GRAD, 512, 384, 1),
     (ACT, 0, 512, 0),
-    (ACT, 512, 512, 1),
+    (ACT, 0, 512, 1),
 )
-EARLY = 3
+AT_ONCE = (0, 1, 2)
+AFTER = {1: (3,), 3: (4, 5)}
 
 
 def pieces_of(m, half):
@@ -50,6 +51,8 @@
     tr = lax.axis_index("tr")
     tc = lax.axis_index("tc")
     is_n = (tr + h) % 2
+    odd = (h + tc) % 2
+    shift = (is_n * odd, (1 - is_n) * odd + is_n * tc)
 
     src = (act, grad)
     out = (out_a, out_g)
@@ -91,12 +94,12 @@
     half_z = z // 2
     c_mine = z % 2
     apart = (half_z + tc) % 2
-    side = (c_mine + apart * tc + (1 - apart) * is_n * h) % 2
+    side = (c_mine + apart * shift[1] + (1 - apart) * shift[0]) % 2
     mirrors = 1 - (1 - is_n) * (1 - apart)
     kind = is_n * (1 + apart)
     turned_rows = (
-        4 * h + 2 * (1 - half_z) + (c_mine + half_z) % 2,
-        4 * (1 - h) + 2 * half_z + (c_mine + 1 - h) % 2,
+        4 * h + 2 * (1 - half_z) + (c_mine + h + half_z) % 2,
+        4 * (1 - h) + 2 * half_z + (c_mine + 1 + h + half_z) % 2,
         4 * (1 - h) + 2 * (1 - half_z) + (c_mine + half_z) % 2,
     )
 
@@ -123,8 +126,10 @@
         copy.start()
     pl.semaphore_wait(barrier, len(peers) + 16 * mirrors)
 
-    def cols(i):
-        return pl.ds(PIECES[i][1], PIECES[i][2])
+    def cols(i, first):
+        m, offset, size, later = PIECES[i]
+        start = (first + later) % 2 * (buf[m].shape[2] // 2) + offset
+        return pl.ds(pl.multiple_of(start, 128), size)
 
     def remote(a, b, ss, rs, to):
         return pltpu.make_async_remote_copy(
@@ -133,24 +138,23 @@
 
     def along_a(i):
         m = PIECES[i][0]
+        to = (1 - is_n) * (1 - odd)
         return remote(
-            src[m].at[:, cols(i)], buf[m].at[1, :, cols(i)], a_send.at[i], a_recv.at[i], x1
+            src[m].at[:, cols(i, to)], buf[m].at[1, :, cols(i, to)], a_send.at[i], a_recv.at[i], x1
         )
 
     def along_b(k, i):
         m = PIECES[i][0]
-        source = src[m].at[:, cols(i)] if k == 0 else buf[m].at[1, :, cols(i)]
-        return remote(
-            source, buf[m].at[3 - k, :, cols(i)], b_send.at[k, i], b_recv.at[k, i], x3
-        )
+        part = cols(i, odd)
+        source = src[m].at[:, part] if k == 0 else buf[m].at[1, :, part]
+        return remote(source, buf[m].at[3 - k, :, part], b_send.at[k, i], b_recv.at[k, i], x3)
 
     def to_core(k, i):
         m = PIECES[i][0]
-        source = src[m].at[:, cols(i)] if k == 0 else buf[m].at[k, :, cols(i)]
+        part = cols(i, 0 if k < 2 else odd)
+        source = src[m].at[:, part] if k == 0 else buf[m].at[k, :, part]
         slot = k + 4 if k < 2 else k
-        return remote(
-            source, buf[m].at[slot, :, cols(i)], d_send.at[k, i], d_recv.at[k, i], core
-        )
+        return remote(source, buf[m].at[slot, :, part], d_send.at[k, i], d_recv.at[k, i], core)
 
     every = range(len(PIECES))
     for i in every:
@@ -158,7 +162,7 @@
 
     @pl.when(is_n == 1)
     def _():
-        for i in range(EARLY):
+        for i in AT_ONCE:
             along_b(0, i).start()
 
     @pl.when(is_n == 0)
@@ -173,8 +177,8 @@
             @pl.when(is_n == 1)
             def _(i=i):
                 along_b(1, i).start()
-                if 1 <= i and i + EARLY - 1 in every:
-                    along_b(0, i + EARLY - 1).start()
+                for j in AFTER.get(i, ()):
+                    along_b(0, j).start()
 
             @pl.when(is_n == 0)
             def _(i=i):
@@ -237,8 +241,9 @@
     def bits_of(yy):
         return ((yy ^ (yy >> 1)) % 2 + ya) % 2, (yy // 2 + yb) % 2
 
-    def product(m, e, c):
-        value = dot(m, e, c, (c + (e * tc if e else is_n * h)) % 2)
+    def product(m, e, order):
+        c = (order + odd) % 2 if e else order
+        value = dot(m, e, c, (c + shift[e]) % 2)
         rows = value.shape[0] // 8
         block = (tc + e) % 2
         rza = (c + block + za) % 2
@@ -255,7 +260,10 @@
                 def _(k=k, q=q):
                     stream_copy(m, k, q, partner(k)).start()
 
-    EXTRA = ((y_a, y_b, z_a), (z_a, y_b, y_a))
+    def pick(a, b):
+        return tuple(v + odd * (w - v) for v, w in zip(a, b))
+
+    EXTRA = ((y_a, y_b, z_a), (pick(z_a, y_b), pick(y_b, z_a), y_a))
 
     def product_extra(m, c):
         value = dot(m, 0, c, 1 - c)
@@ -264,7 +272,7 @@
         for yy in range(4):
             rya, ryb = bits_of(yy)
             for k in range(2):
-                q = rya + 2 * ryb + 4 * rza if k == 0 else rza + 2 * ryb + 4 * rya
+                q = rya + 2 * ryb + 4 * rza if k == 0 else (1 + odd) * rza + (2 - odd) * ryb + 4 * rya
                 first = (2 * yy + k) * rows
                 prox[m][k, q] = value[first : first + rows].astype(jnp.bfloat16)
 
@@ -278,20 +286,37 @@
             value = value + got_ref[k, p].astype(jnp.float32)
         return value
 
-    def stage(m, j):
-        for k in range(2):
-            to = partner((j + k) % 4)
-
-            def one(i, carry, k=k, to=to):
-                q = i * 2 ** (j + 1) + 2**j
-                parts = [q + 2**b for b in range(j)]
-                for p in parts:
-                    stream_copy(m, k, p, core).wait_recv()
-                prod[m][k, q] = total(prod[m], recv[m], k, q, parts).astype(jnp.bfloat16)
-                stream_copy(m, k, q, to).start()
-                return carry
-
-            lax.fori_loop(0, 2 ** (3 - j), one, 0)
+    early_0 = 1
+    early_1 = 1 - is_n * tc
+
+    def is_early(k, q):
+        def bit(d0, d1):
+            at0, at1 = 2 ** ((d0 - k) % 4), 2 ** ((d1 - k) % 4)
+            return (1 - tr) * (q // at0 % 2) + tr * (q // at1 % 2)
+
+        block = (bit(3, 1) + zb) % 2
+        c = (bit(2, 0) + za + block) % 2
+        e = (block + tc) % 2
+        return (1 - e) * (1 - c) + e * ((c + odd + 1) % 2) * early_1
+
+    def stage(m, j, early=None):
+        def move(k, q, parts):
+            for p in parts:
+                stream_copy(m, k, p, core).wait_recv()
+            prod[m][k, q] = total(prod[m], recv[m], k, q, parts).astype(jnp.bfloat16)
+            stream_copy(m, k, q, partner((j + k) % 4)).start()
+
+        def one(i, carry):
+            q = i * 2 ** (j + 1) + 2**j
+            parts = [q + 2**b for b in range(j)]
+            for k in range(2):
+                if early is None:
+                    move(k, q, parts)
+                else:
+                    pl.when(is_early(k, q) == early)(functools.partial(move, k, q, parts))
+            return carry
+
+        lax.fori_loop(0, 2 ** (3 - j), one, 0)
 
     def stage_extra(m, j):
         @pl.when(is_n == 0)
@@ -447,9 +472,6 @@
     finish_extra = scoped("finish_extra", finish_extra)
     gather_rows = scoped("gather_rows", gather_rows)
 
-    early_0 = 1 - is_n * h
-    early_1 = 1 - tc
-
     for copy in own:
         copy.wait()
     step_a(GRAD, 0)
@@ -460,26 +482,27 @@
     products(GRAD, 0, early_0, 2)
     products(GRAD, 1, early_1, 1)
     extras(GRAD)
+    stage(GRAD, 1, 1)
     step_b(GRAD, 1)
     products(GRAD, 1, 1, 2)
     step_a(ACT, 0)
-    stage(GRAD, 1)
-    stage_extra(GRAD, 1)
     step_a(ACT, 1)
     products(ACT, 0, 0, 2)
     extras(ACT)
-    stage(GRAD, 2)
-    stage_extra(GRAD, 2)
+    stage(GRAD, 1, 0)
+    stage_extra(GRAD, 1)
     step_b(ACT, 0)
     step_b(ACT, 1)
     products(ACT, 1, 0, 2)
+    stage(GRAD, 2)
+    stage_extra(GRAD, 2)
+    stage(ACT, 1)
+    stage_extra(ACT, 1)
     stage(GRAD, 3)
     stage_extra(GRAD, 3)
-    stage(ACT, 1)
-    stage_extra(ACT, 1)
-    finish(GRAD)
     stage(ACT, 2)
     stage_extra(ACT, 2)
+    finish(GRAD)
     finish_extra(GRAD)
     stage(ACT, 3)
     stage_extra(ACT, 3)

time: 147 us -> 133 us (0.905)
  Pallas kernels: 142 us -> 128 us
    pallas_call x1, Pallas kernels: 142 us -> 128 us  [sums(): pl.pallas_call(kernel, out_shape=[jax.ShapeDtypeStruct((r, 4 * w), bf16)...]
where the time goes in v3:
time: 133 us
  Pallas kernels  128 us (96%)
  other arithmetic  3.96 us (3%)
    pallas_call x1, Pallas kernels, sums(): pl.pallas_call(kernel, out_shape=[jax.ShapeDtypeStruct((r, 4 * w), bf16)...  128 us
    add x1, other arithmetic, body(): 0.5 * old_gradients + scale * sum_g.astype(jnp.float32)  3.09 us

profile of v3, /device:TPU:1, one launch (start us, length us, event | category | flops | bytes accessed | tf_op | source)
XLA Modules:
  0.0 132.7 jit_solution(240507645551250990)
XLA Ops:
  0.6 128.1 %shard_map.59 = (bf16[32,4096]{1,0:T(8,128)(2,1)}, bf16[56,7168]{1,0:T(8,128)(2,1)}) custom-call(bf16[512,1024]{1,0:T(8,128)(2,1)} %act.1, bf16[512,1792]{1,0:T(8,128)(2,1)} %grad.1), custom_call_target="tpu_custom_call" | custom-call | tf_op jit(solution)/shard_map/pallas_call | solution.py:585
  128.7 0.0 copy-start
  128.8 0.0 copy-start.1
  128.8 3.1 %multiply_add_fusion = f32[56,7168]{1,0:T(8,128)} fusion(bf16[56,7168]{1,0:T(8,128)(2,1)} %get-tuple-element.5, f32[56,7168]{1,0:T(8,128)} %param.7), kind=kLoop, calls=%fused_computation | loop fusion | flops 1605632 | bytes 4014080 | tf_op jit(solution)/shard_map/add | solution.py:603
  131.9 0.0 copy-done
  131.9 0.0 copy-done.1
  131.9 0.9 multiply_add_fusion.1
Async XLA Ops:
  128.7 3.1 %copy-start = (f32[32,4096]{1,0:T(8,128)S(1)}, f32[32,4096]{1,0:T(8,128)}, u32[]{:S(2)}) copy-start(f32[32,4096]{1,0:T(8,128)} %param.6) | copy-start | bytes 1572868
  128.8 3.1 %copy-start.1 = (bf16[32,4096]{1,0:T(8,128)(2,1)S(1)}, bf16[32,4096]{1,0:T(8,128)(2,1)}, u32[]{:S(2)}) copy-start(bf16[32,4096]{1,0:T(8,128)(2,1)} %get-tuple-element.4) | copy-start | bytes 786436

commit v4 on v3

--- a/solution.py
+++ b/solution.py
@@ -117,14 +117,11 @@
 
     for peer in peers:
         greet(peer)
-    for chunk in turned_rows:
-        for yy in range(4):
-            greet((chunk // 4, chunk % 4, yy, h, half_z))
 
     own = [pltpu.make_async_copy(src[m], buf[m].at[0], own_sem.at[m]) for m in (ACT, GRAD)]
     for copy in own:
         copy.start()
-    pl.semaphore_wait(barrier, len(peers) + 16 * mirrors)
+    pl.semaphore_wait(barrier, len(peers))
 
     def cols(i, first):
         m, offset, size, later = PIECES[i]
@@ -585,11 +582,11 @@
     return pl.pallas_call(
         kernel,
         out_shape=[jax.ShapeDtypeStruct((r, 4 * w), bf16) for r, w in zip(rows, wide)],
-        in_specs=[anywhere] * 2,
+        in_specs=[pl.BlockSpec(memory_space=pltpu.HBM)] * 2,
         out_specs=[anywhere] * 2,
         scratch_shapes=[*vmem, *sems],
         compiler_params=pltpu.CompilerParams(
-            collective_id=0, has_side_effects=True, vmem_limit_bytes=66_000_000
+            collective_id=0, has_side_effects=True, vmem_limit_bytes=53_500_000
         ),
     )(activations, gradients)
 

time: 133 us -> 131 us (0.985)
  other arithmetic: 3.96 us -> 2.24 us
    add x1, other arithmetic: 3.09 us -> 1.36 us  [body(): 0.5 * old_gradients + scale * sum_g.astype(jnp.float32)]
where the time goes in v4:
time: 131 us
  Pallas kernels  127 us (97%)
  other arithmetic  2.24 us (2%)
    pallas_call x1, Pallas kernels, sums(): pl.pallas_call(kernel, out_shape=[jax.ShapeDtypeStruct((r, 4 * w), bf16)...  127 us

profile of v4, /device:TPU:1, one launch (start us, length us, event | category | flops | bytes accessed | tf_op | source)
XLA Modules:
  0.0 131.1 jit_solution(1799655156557056218)
XLA Ops:
  0.6 0.0 copy-start
  0.6 1.2 copy-done
  1.9 0.0 copy-start.1
  1.9 127.0 %shard_map.59 = (bf16[32,4096]{1,0:T(8,128)(2,1)S(1)}, bf16[56,7168]{1,0:T(8,128)(2,1)S(1)}) custom-call(bf16[512,1024]{1,0:T(8,128)(2,1)S(1)} %copy-done, bf16[512,1792]{1,0:T(8,128)(2,1)} %grad.1), custom_call_target="tpu_custom_call" | custom-call | tf_op jit(solution)/shard_map/pallas_call | solution.py:582
  128.8 0.0 copy-done.1
  128.8 0.0 copy-start.2
  128.9 1.4 %multiply_add_fusion = f32[56,7168]{1,0:T(8,128)} fusion(bf16[56,7168]{1,0:T(8,128)(2,1)S(1)} %get-tuple-element.5, f32[56,7168]{1,0:T(8,128)S(1)} %copy-done.1), kind=kLoop, calls=%fused_computation | loop fusion | flops 1605632 | bytes 4014080 | tf_op jit(solution)/shard_map/add | solution.py:600
  130.2 0.0 copy-done.2
  130.2 0.9 multiply_add_fusion.1
Async XLA Ops:
  0.6 1.2 copy-start
  1.9 127.0 %copy-start.1 = (f32[56,7168]{1,0:T(8,128)S(1)}, f32[56,7168]{1,0:T(8,128)}, u32[]{:S(2)}) copy-start(f32[56,7168]{1,0:T(8,128)} %param.7) | copy-start | bytes 4816900
  128.8 1.4 %copy-start.2 = (f32[32,4096]{1,0:T(8,128)S(1)}, f32[32,4096]{1,0:T(8,128)}, u32[]{:S(2)}) copy-start(f32[32,4096]{1,0:T(8,128)} %param.6) | copy-start | bytes 1572868

commit v5 on v4

--- a/solution.py
+++ b/solution.py
@@ -41,9 +41,11 @@
 def kernel(
     act, grad, out_a, out_g,
     buf_a, buf_g, prod_a, prod_g, recv_a, recv_g, prox_a, prox_g, recx_a, recx_g,
-    fin_a, fin_g, finx_a, finx_g, turn_a, turn_g, mir_a, mir_g, row_a, row_g,
+    fin_a, fin_g, finx_a, finx_g, turn_a, turn_g, turx_a, turx_g,
+    mir_a, mir_g, mirx_a, mirx_g, row_a, row_g,
     own_sem, a_send, a_recv, b_send, b_recv, d_send, d_recv,
-    s_send, s_recv, x_send, x_recv, f_send, f_recv, g_send, g_recv, m_send, m_recv, o_sem,
+    s_send, s_recv, x_send, x_recv, f_send, f_recv, g_send, g_recv,
+    m_send, m_recv, n_send, n_recv, o_sem,
 ):
     h = lax.axis_index("dp_0")
     z = lax.axis_index("dp_1")
@@ -64,7 +66,9 @@
     fin = (fin_a, fin_g)
     finx = (finx_a, finx_g)
     turn = (turn_a, turn_g)
+    turx = (turx_a, turx_g)
     mir = (mir_a, mir_g)
+    mirx = (mirx_a, mirx_g)
     row = (row_a, row_g)
 
     def flip1(v):
@@ -137,21 +141,21 @@
         m = PIECES[i][0]
         to = (1 - is_n) * (1 - odd)
         return remote(
-            src[m].at[:, cols(i, to)], buf[m].at[1, :, cols(i, to)], a_send.at[i], a_recv.at[i], x1
+            src[m].at[:, cols(i, to)], buf[m].at[1, :, cols(i, to)], a_send.at[m], a_recv.at[i], x1
         )
 
     def along_b(k, i):
         m = PIECES[i][0]
         part = cols(i, odd)
         source = src[m].at[:, part] if k == 0 else buf[m].at[1, :, part]
-        return remote(source, buf[m].at[3 - k, :, part], b_send.at[k, i], b_recv.at[k, i], x3)
+        return remote(source, buf[m].at[3 - k, :, part], b_send.at[k, m], b_recv.at[k, i], x3)
 
     def to_core(k, i):
         m = PIECES[i][0]
         part = cols(i, 0 if k < 2 else odd)
         source = src[m].at[:, part] if k == 0 else buf[m].at[k, :, part]
         slot = k + 4 if k < 2 else k
-        return remote(source, buf[m].at[slot, :, part], d_send.at[k, i], d_recv.at[k, i], core)
+        return remote(source, buf[m].at[slot, :, part], d_send.at[k, m], d_recv.at[k, i], core)
 
     every = range(len(PIECES))
     for i in every:
@@ -214,12 +218,21 @@
 
     def stream_copy(m, k, q, to):
         return remote(
-            prod[m].at[k, q], recv[m].at[k, q], s_send.at[m, k, q], s_recv.at[m, k, q], to
-        )
+            prod[m].at[k, q], recv[m].at[k, q], s_send.at[m, k], s_recv.at[m, k, q], to
+        )
+
+    def lanes_of(m, k):
+        tiles = buf[m].shape[2] // 256
+        first = (tiles + 1) // 2 * 128
+        return pl.ds(0, first) if k == 0 else pl.ds(first, tiles * 128 - first)
 
     def extra_copy(m, k, q, to):
         return remote(
-            prox[m].at[k, q], recx[m].at[k, q], x_send.at[m, k, q], x_recv.at[m, k, q], to
+            prox[m].at[q, :, lanes_of(m, k)],
+            recx[m].at[q, :, lanes_of(m, k)],
+            x_send.at[m, k],
+            x_recv.at[m, k, q],
+            to,
         )
 
     def dot(m, e, c, s):
@@ -257,25 +270,29 @@
                 def _(k=k, q=q):
                     stream_copy(m, k, q, partner(k)).start()
 
-    def pick(a, b):
-        return tuple(v + odd * (w - v) for v, w in zip(a, b))
-
-    EXTRA = ((y_a, y_b, z_a), (pick(z_a, y_b), pick(y_b, z_a), y_a))
-
-    def product_extra(m, c):
-        value = dot(m, 0, c, 1 - c)
-        rows = value.shape[0] // 8
-        rza = (c + tc + za) % 2
+    EXTRA = ((y_a, y_b, z_a, z_b), (z_b, z_a, y_b, y_a))
+
+    def product_extra(m):
+        value = dot(m, 0, 0, 1)
+        rows = value.shape[0] // 16
         for yy in range(4):
             rya, ryb = bits_of(yy)
-            for k in range(2):
-                q = rya + 2 * ryb + 4 * rza if k == 0 else (1 + odd) * rza + (2 - odd) * ryb + 4 * rya
-                first = (2 * yy + k) * rows
-                prox[m][k, q] = value[first : first + rows].astype(jnp.bfloat16)
-
-                @pl.when(q % 2 == 1)
-                def _(k=k, q=q):
-                    extra_copy(m, k, q, EXTRA[k][0]).start()
+            for zz in range(4):
+                rza = ((zz ^ (zz >> 1)) % 2 + za) % 2
+                rzb = (zz // 2 + zb) % 2
+                first = (4 * yy + zz) * rows
+                part = value[first : first + rows].astype(jnp.bfloat16)
+                for k in range(2):
+                    if k == 0:
+                        q = rya + 2 * ryb + 4 * rza + 8 * rzb
+                    else:
+                        q = rzb + 2 * rza + 4 * ryb + 8 * rya
+                    lanes = lanes_of(m, k)
+                    prox[m][q, :, lanes] = part[:, lanes.start : lanes.start + lanes.size]
+
+                    @pl.when(q % 2 == 1)
+                    def _(k=k, q=q):
+                        extra_copy(m, k, q, EXTRA[k][0]).start()
 
     def total(own_ref, got_ref, k, q, parts):
         value = own_ref[k, q].astype(jnp.float32)
@@ -315,34 +332,26 @@
 
         lax.fori_loop(0, 2 ** (3 - j), one, 0)
 
+    def total_extra(m, k, q, parts):
+        for p in parts:
+            extra_copy(m, k, p, core).wait_recv()
+        value = prox[m][q, :, lanes_of(m, k)].astype(jnp.float32)
+        for p in parts:
+            value = value + recx[m][p, :, lanes_of(m, k)].astype(jnp.float32)
+        return value
+
     def stage_extra(m, j):
+        def one(i, carry):
+            q = i * 2 ** (j + 1) + 2**j
+            parts = [q + 2**b for b in range(j)]
+            for k in range(2):
+                prox[m][q, :, lanes_of(m, k)] = total_extra(m, k, q, parts).astype(jnp.bfloat16)
+                extra_copy(m, k, q, EXTRA[k][j]).start()
+            return carry
+
         @pl.when(is_n == 0)
         def _():
-            for k in range(2):
-                if j < 3:
-
-                    def one(i, carry, k=k):
-                        q = i * 2 ** (j + 1) + 2**j
-                        parts = [q + 2**b for b in range(j)]
-                        for p in parts:
-                            extra_copy(m, k, p, core).wait_recv()
-                        prox[m][k, q] = total(prox[m], recx[m], k, q, parts).astype(
-                            jnp.bfloat16
-                        )
-                        extra_copy(m, k, q, EXTRA[k][j]).start()
-                        return carry
-
-                    lax.fori_loop(0, 2 ** (2 - j), one, 0)
-                else:
-                    for p in (1, 2, 4):
-                        extra_copy(m, k, p, core).wait_recv()
-
-                    @pl.when(apart == 1)
-                    def _(k=k):
-                        prox[m][k, 0] = total(prox[m], recx[m], k, 0, (1, 2, 4)).astype(
-                            jnp.bfloat16
-                        )
-                        extra_copy(m, k, 0, z_b).start()
+            lax.fori_loop(0, 2 ** (3 - j), one, 0)
 
     def at(m, block, s):
         width = buf[m].shape[2]
@@ -355,24 +364,32 @@
         return remote(
             fin[m].at[2 * to[3] + to[4]],
             row[m].at[:, at(m, 2 * tr + tc, side)],
-            f_send.at[m, k],
+            f_send.at[m],
             f_recv.at[m, k],
             to,
         )
 
-    def last_extra(m, k):
-        to = others[k]
+    extra_to = (h, 2 * tc, y, half_z, c_mine)
+    keeps = (1 - is_n) * (1 - apart) * (1 - c_mine) * (1 - tr) * (1 - tc)
+    keeps_turned = (1 - is_n) * (1 - apart) * c_mine
+
+    def last_extra(m):
         return remote(
-            finx[m].at[2 * to[3] + to[4]],
-            row[m].at[:, at(m, 2 * tr + tc, 1 - c_mine)],
-            g_send.at[m, k],
-            g_recv.at[m],
-            to,
-        )
+            finx[m], row[m].at[:, at(m, 2 * tr + tc, 1)], g_send.at[m], g_recv.at[m], extra_to
+        )
+
+    def turned_extra(m, i):
+        to = (h, 2 * tc + 1, i // 4, i // 2 % 2, i % 2)
+        return remote(
+            turx[m].at[i], mirx[m].at[4 * y + z], n_send.at[m], n_recv.at[m], to
+        )
+
+    def is_self(i):
+        return keeps_turned * (i == 4 * y + 2 * tr + tc).astype(jnp.int32)
 
     def turned_copy(m, i, to):
         return remote(
-            turn[m].at[i], mir[m].at[kind, y], m_send.at[m, i], m_recv.at[m, kind, y], to
+            turn[m].at[i], mir[m].at[kind, y], m_send.at[m], m_recv.at[m, kind], to
         )
 
     def by_quarter(m, ref, value, s):
@@ -407,25 +424,41 @@
                 turned_copy(m, i, to).start()
 
     def finish_extra(m):
-        @pl.when(mirrors == 0)
-        def _():
-            for k in range(2):
-                extra_copy(m, k, 0, core).wait_recv()
+        @pl.when(is_n == 0)
+        def _():
             value = jnp.concatenate(
-                [total(prox[m], recx[m], k, 0, (1, 2, 4, 0)) for k in range(2)], axis=0
+                [total_extra(m, k, 0, (1, 2, 4, 8)) for k in range(2)], axis=1
             )
-            by_quarter(m, finx, value, 1 - c_mine)
-            for k in range(3):
-                last_extra(m, k).start()
+            finx[m][...] = value.astype(jnp.bfloat16)
+
+            @pl.when(keeps == 0)
+            def _():
+                last_extra(m).start()
+
+            @pl.when(keeps == 1)
+            def _():
+                row[m][:, at(m, 2 * tr + tc, 1)] = finx[m][...]
+
+            rows = value.shape[0]
+            fill = jnp.zeros((128 - rows, value.shape[1]), jnp.float32)
+            turned = jnp.concatenate([value, fill], axis=0).T
+            for i in range(16):
+                turx[m][i] = turned[i * rows : (i + 1) * rows].astype(jnp.bfloat16)
+
+                @pl.when(is_self(i) == 0)
+                def _(i=i):
+                    turned_extra(m, i).start()
+
+                @pl.when(is_self(i) == 1)
+                def _(i=i):
+                    mirx[m][4 * y + z] = turx[m][i]
 
     def gather_rows(m):
         width = buf[m].shape[2]
         rows = width // 8
         for t in range(3):
-            for yy in range(4):
-                remote(
-                    turn[m].at[0], mir[m].at[t, yy], m_send.at[m, 0], m_recv.at[m, t, yy], core
-                ).wait_recv()
+            pieces = mir[m].at[t]
+            remote(pieces, pieces, m_send.at[m], m_recv.at[m, t], core).wait_recv()
             value = jnp.concatenate(
                 [mir[m][t, yy].astype(jnp.float32)[:, :rows] for yy in range(4)], axis=1
             )
@@ -434,9 +467,24 @@
         for k in range(3):
             last_copy(m, k).wait_recv()
 
-        @pl.when(mirrors == 1)
-        def _():
-            last_extra(m, 0).wait_recv()
+        @pl.when(c_mine * (1 - keeps) + (1 - c_mine) * keeps == 0)
+        def _():
+            last_extra(m).wait_recv()
+
+        @pl.when(c_mine == 1)
+        def _():
+            rows = width // 32
+            for count in (15, 16):
+
+                @pl.when(keeps_turned == 16 - count)
+                def _(count=count):
+                    pieces = mirx[m].at[pl.ds(0, count)]
+                    remote(pieces, pieces, n_send.at[m], n_recv.at[m], core).wait_recv()
+
+            value = jnp.concatenate(
+                [mirx[m][i].astype(jnp.float32)[:, :rows] for i in range(16)], axis=1
+            )
+            row[m][:, at(m, 2 * h + half_z, 0)] = value.astype(jnp.bfloat16)
 
         own_out(m).start()
 
@@ -453,11 +501,7 @@
     def extras(m):
         @pl.when(is_n == 0)
         def _():
-            def one(c, carry):
-                product_extra(m, c)
-                return carry
-
-            lax.fori_loop(0, 2, one, 0)
+            product_extra(m)
 
     step_a = scoped("step_a", step_a)
     step_b = scoped("step_b", step_b)
@@ -497,9 +541,9 @@
     stage_extra(ACT, 1)
     stage(GRAD, 3)
     stage_extra(GRAD, 3)
+    finish(GRAD)
     stage(ACT, 2)
     stage_extra(ACT, 2)
-    finish(GRAD)
     finish_extra(GRAD)
     stage(ACT, 3)
     stage_extra(ACT, 3)
@@ -509,45 +553,42 @@
     gather_rows(ACT)
 
     with jax.named_scope("drain"):
-        for i in every:
-            along_a(i).wait_send()
-
-        @pl.when(is_n == 1)
-        def _():
-            for i in every:
+        def sent(ref, sem):
+            pltpu.make_async_copy(ref, ref, sem).wait()
+
+        for m in (ACT, GRAD):
+            block = buf[m].at[1]
+            sent(block, a_send.at[m])
+
+            @pl.when(is_n == 1)
+            def _(m=m, block=block):
                 for k in (0, 1):
-                    along_b(k, i).wait_send()
-
-        @pl.when(is_n == 0)
-        def _():
-            for i in every:
+                    sent(block, b_send.at[k, m])
+
+            @pl.when(is_n == 0)
+            def _(m=m, block=block):
                 for k in range(4):
-                    to_core(k, i).wait_send()
-            for m in (ACT, GRAD):
+                    sent(block, d_send.at[k, m])
                 for k in range(2):
-                    for q in range(1, 8):
-                        extra_copy(m, k, q, core).wait_send()
-
-                    @pl.when(apart == 1)
-                    def _(m=m, k=k):
-                        extra_copy(m, k, 0, core).wait_send()
-
-        for m in (ACT, GRAD):
+                    sent(prox[m].at[pl.ds(1, 15), :, lanes_of(m, k)], x_send.at[m, k])
+
+                @pl.when(keeps == 0)
+                def _():
+                    last_extra(m).wait_send()
+
+                for count in (15, 16):
+
+                    @pl.when(keeps_turned == 16 - count)
+                    def _(count=count):
+                        sent(turx[m].at[pl.ds(0, count)], n_send.at[m])
+
             for k in range(2):
-                for q in range(1, 16):
-                    stream_copy(m, k, q, core).wait_send()
-            for k in range(3):
-                last_copy(m, k).wait_send()
+                sent(prod[m].at[k, pl.ds(1, 15)], s_send.at[m, k])
+            sent(fin[m].at[pl.ds(0, 3)], f_send.at[m])
 
             @pl.when(mirrors == 1)
             def _(m=m):
-                for i, to in quarters():
-                    turned_copy(m, i, to).wait_send()
-
-            @pl.when(mirrors == 0)
-            def _(m=m):
-                for k in range(3):
-                    last_extra(m, k).wait_send()
+                sent(turn[m], m_send.at[m])
 
             own_out(m).wait()
 
@@ -562,21 +603,23 @@
         *(pltpu.VMEM((6, tokens, w), bf16) for w in wide),
         *(pltpu.VMEM((2, 16, w // 16, w // 2), bf16) for w in wide),
         *(pltpu.VMEM((2, 16, w // 16, w // 2), bf16) for w in wide),
-        *(pltpu.VMEM((2, 8, w // 16, w // 2), bf16) for w in wide),
-        *(pltpu.VMEM((2, 8, w // 16, w // 2), bf16) for w in wide),
+        *(pltpu.VMEM((16, r, w // 2), bf16) for r, w in zip(rows, wide)),
+        *(pltpu.VMEM((16, r, w // 2), bf16) for r, w in zip(rows, wide)),
         *(pltpu.VMEM((4, r, w // 2), bf16) for r, w in zip(rows, wide)),
-        *(pltpu.VMEM((4, r, w // 2), bf16) for r, w in zip(rows, wide)),
+        *(pltpu.VMEM((r, w // 2), bf16) for r, w in zip(rows, wide)),
         *(pltpu.VMEM((16, r, n), bf16) for r, n in zip(rows, lanes)),
+        *(pltpu.VMEM((16, r, 128), bf16) for r in rows),
         *(pltpu.VMEM((3, 4, r, n), bf16) for r, n in zip(rows, lanes)),
+        *(pltpu.VMEM((16, r, 128), bf16) for r in rows),
         *(pltpu.VMEM((r, 4 * w), bf16) for r, w in zip(rows, wide)),
     ]
     n = len(PIECES)
     dma = pltpu.SemaphoreType.DMA
     sems = [
-        dma((2,)), dma((n,)), dma((n,)), dma((2, n)), dma((2, n)), dma((4, n)), dma((4, n)),
-        dma((2, 2, 16)), dma((2, 2, 16)), dma((2, 2, 8)), dma((2, 2, 8)),
-        dma((2, 3)), dma((2, 3)), dma((2, 3)), dma((2,)),
-        dma((2, 16)), dma((2, 3, 4)), dma((2,)),
+        dma((2,)), dma((2,)), dma((n,)), dma((2, 2)), dma((2, n)), dma((4, 2)), dma((4, n)),
+        dma((2, 2)), dma((2, 2, 16)), dma((2, 2)), dma((2, 2, 16)),
+        dma((2,)), dma((2, 3)), dma((2,)), dma((2,)),
+        dma((2,)), dma((2, 3)), dma((2,)), dma((2,)), dma((2,)),
     ]
     anywhere = pl.BlockSpec(memory_space=pl.ANY)
     return pl.pallas_call(
@@ -586,7 +629,7 @@
         out_specs=[anywhere] * 2,
         scratch_shapes=[*vmem, *sems],
         compiler_params=pltpu.CompilerParams(
-            collective_id=0, has_side_effects=True, vmem_limit_bytes=53_500_000
+            collective_id=0, has_side_effects=True, vmem_limit_bytes=54_800_000
         ),
     )(activations, gradients)
 

time: 131 us -> 132 us (level)
  Pallas kernels: 127 us -> 129 us
    pallas_call x1, Pallas kernels: 127 us -> 129 us  [sums(): pl.pallas_call(kernel, out_shape=[jax.ShapeDtypeStruct((r, 4 * w), bf16)...]
where the time goes in v5:
time: 132 us
  Pallas kernels  129 us (98%)
  other arithmetic  2.23 us (2%)
    pallas_call x1, Pallas kernels, sums(): pl.pallas_call(kernel, out_shape=[jax.ShapeDtypeStruct((r, 4 * w), bf16)...  129 us

profile of v5, /device:TPU:1, one launch (start us, length us, event | category | flops | bytes accessed | tf_op | source)
XLA Modules:
  0.0 131.6 jit_solution(16587206091432395901)
XLA Ops:
  0.6 0.0 copy-start
  0.6 128.7 %shard_map.59 = (bf16[32,4096]{1,0:T(8,128)(2,1)S(1)}, bf16[56,7168]{1,0:T(8,128)(2,1)S(1)}) custom-call(bf16[512,1024]{1,0:T(8,128)(2,1)} %act.1, bf16[512,1792]{1,0:T(8,128)(2,1)} %grad.1), custom_call_target="tpu_custom_call" | custom-call | tf_op jit(solution)/shard_map/pallas_call | solution.py:625
  129.4 0.0 copy-done
  129.4 0.0 copy-start.1
  129.4 1.4 %multiply_add_fusion = f32[56,7168]{1,0:T(8,128)} fusion(bf16[56,7168]{1,0:T(8,128)(2,1)S(1)} %get-tuple-element.5, f32[56,7168]{1,0:T(8,128)S(1)} %copy-done), kind=kLoop, calls=%fused_computation | loop fusion | flops 1605632 | bytes 4014080 | tf_op jit(solution)/shard_map/add | solution.py:643
  130.8 0.0 copy-done.1
  130.8 0.9 multiply_add_fusion.1
Async XLA Ops:
  0.6 128.7 %copy-start = (f32[56,7168]{1,0:T(8,128)S(1)}, f32[56,7168]{1,0:T(8,128)}, u32[]{:S(2)}) copy-start(f32[56,7168]{1,0:T(8,128)} %param.7) | copy-start | bytes 4816900
  129.4 1.4 %copy-start.1 = (f32[32,4096]{1,0:T(8,128)S(1)}, f32[32,4096]{1,0:T(8,128)}, u32[]{:S(2)}) copy-start(f32[32,4096]{1,0:T(8,128)} %param.6) | copy-start | bytes 1572868

commit v6 on v5

--- a/solution.py
+++ b/solution.py
@@ -17,13 +17,14 @@
 PIECES = (
     (GRAD, 0, 512, 0),
     (GRAD, 512, 384, 0),
-    (GRAD, 0, 512, 1),
-    (GRAD, 512, 384, 1),
+    (GRAD, 0, 384, 1),
+    (GRAD, 384, 256, 1),
+    (GRAD, 640, 256, 1),
     (ACT, 0, 512, 0),
     (ACT, 0, 512, 1),
 )
 AT_ONCE = (0, 1, 2)
-AFTER = {1: (3,), 3: (4, 5)}
+AFTER = {1: (3, 4), 4: (5, 6)}
 
 
 def pieces_of(m, half):
@@ -54,7 +55,7 @@
     tc = lax.axis_index("tc")
     is_n = (tr + h) % 2
     odd = (h + tc) % 2
-    shift = (is_n * odd, (1 - is_n) * odd + is_n * tc)
+    shift = (is_n * odd, (1 - is_n) * odd + is_n * h)
 
     src = (act, grad)
     out = (out_a, out_g)
@@ -86,7 +87,7 @@
 
     def partner(d):
         f = flip1 if d % 2 == 0 else flip3
-        on_y = (1 - tr) if d < 2 else tr
+        on_y = is_n if d < 2 else 1 - is_n
         return (
             h,
             on_y * z + (1 - on_y) * f(z),
@@ -104,7 +105,7 @@
     turned_rows = (
         4 * h + 2 * (1 - half_z) + (c_mine + h + half_z) % 2,
         4 * (1 - h) + 2 * half_z + (c_mine + 1 + h + half_z) % 2,
-        4 * (1 - h) + 2 * (1 - half_z) + (c_mine + half_z) % 2,
+        4 * (1 - h) + 2 * (1 - half_z) + (c_mine + 1 + h) % 2,
     )
 
     def quarters():
@@ -214,7 +215,7 @@
 
     def weight(d0, d1, k):
         on0, on1 = 2 ** ((d0 - k) % 4), 2 ** ((d1 - k) % 4)
-        return on0 + tr * (on1 - on0)
+        return on0 + (1 - is_n) * (on1 - on0)
 
     def stream_copy(m, k, q, to):
         return remote(
@@ -301,19 +302,20 @@
         return value
 
     early_0 = 1
-    early_1 = 1 - is_n * tc
-
-    def is_early(k, q):
+    early_1 = 1 - is_n * h
+
+    def group_of(k, q):
         def bit(d0, d1):
             at0, at1 = 2 ** ((d0 - k) % 4), 2 ** ((d1 - k) % 4)
-            return (1 - tr) * (q // at0 % 2) + tr * (q // at1 % 2)
+            return is_n * (q // at0 % 2) + (1 - is_n) * (q // at1 % 2)
 
         block = (bit(3, 1) + zb) % 2
         c = (bit(2, 0) + za + block) % 2
         e = (block + tc) % 2
-        return (1 - e) * (1 - c) + e * ((c + odd + 1) % 2) * early_1
-
-    def stage(m, j, early=None):
+        second = (c + odd) % 2
+        return (1 - e) * c + e * (2 * second + (1 - second) * (1 - early_1))
+
+    def stage(m, j, group=None):
         def move(k, q, parts):
             for p in parts:
                 stream_copy(m, k, p, core).wait_recv()
@@ -324,10 +326,10 @@
             q = i * 2 ** (j + 1) + 2**j
             parts = [q + 2**b for b in range(j)]
             for k in range(2):
-                if early is None:
+                if group is None:
                     move(k, q, parts)
                 else:
-                    pl.when(is_early(k, q) == early)(functools.partial(move, k, q, parts))
+                    pl.when(group_of(k, q) == group)(functools.partial(move, k, q, parts))
             return carry
 
         lax.fori_loop(0, 2 ** (3 - j), one, 0)
@@ -421,6 +423,11 @@
             rows = turned.shape[0] // 16
             for i, to in quarters():
                 turn[m][i] = turned[i * rows : (i + 1) * rows].astype(jnp.bfloat16)
+
+    def send_turned(m):
+        @pl.when(mirrors == 1)
+        def _():
+            for i, to in quarters():
                 turned_copy(m, i, to).start()
 
     def finish_extra(m):
@@ -512,6 +519,7 @@
     finish = scoped("finish", finish)
     finish_extra = scoped("finish_extra", finish_extra)
     gather_rows = scoped("gather_rows", gather_rows)
+    send_turned = scoped("send_turned", send_turned)
 
     for copy in own:
         copy.wait()
@@ -523,15 +531,17 @@
     products(GRAD, 0, early_0, 2)
     products(GRAD, 1, early_1, 1)
     extras(GRAD)
-    stage(GRAD, 1, 1)
+    stage(GRAD, 1, 0)
     step_b(GRAD, 1)
     products(GRAD, 1, 1, 2)
     step_a(ACT, 0)
+    products(ACT, 0, 0, 1)
+    stage(GRAD, 1, 1)
+    stage_extra(GRAD, 1)
     step_a(ACT, 1)
-    products(ACT, 0, 0, 2)
+    products(ACT, 0, 1, 2)
     extras(ACT)
-    stage(GRAD, 1, 0)
-    stage_extra(GRAD, 1)
+    stage(GRAD, 1, 2)
     step_b(ACT, 0)
     step_b(ACT, 1)
     products(ACT, 1, 0, 2)
@@ -541,13 +551,15 @@
     stage_extra(ACT, 1)
     stage(GRAD, 3)
     stage_extra(GRAD, 3)
-    finish(GRAD)
     stage(ACT, 2)
     stage_extra(ACT, 2)
-    finish_extra(GRAD)
+    finish(GRAD)
     stage(ACT, 3)
     stage_extra(ACT, 3)
+    send_turned(GRAD)
+    finish_extra(GRAD)
     finish(ACT)
+    send_turned(ACT)
     finish_extra(ACT)
     gather_rows(GRAD)
     gather_rows(ACT)

time: 132 us -> 126 us (0.955)
  the two profiles are of different devices: /device:TPU:1 before, /device:TPU:97 now
where the time goes in v6:
time: 126 us
  Pallas kernels  123 us (98%)
  other arithmetic  2.23 us (2%)
    pallas_call x1, Pallas kernels, sums(): pl.pallas_call(kernel, out_shape=[jax.ShapeDtypeStruct((r, 4 * w), bf16)...  123 us

profile of v6, /device:TPU:97, one launch (start us, length us, event | category | flops | bytes accessed | tf_op | source)
XLA Modules:
  0.0 125.7 jit_solution(15932704619998382984)
XLA Ops:
  0.6 0.0 copy-start
  0.6 122.8 %shard_map.59 = (bf16[32,4096]{1,0:T(8,128)(2,1)S(1)}, bf16[56,7168]{1,0:T(8,128)(2,1)S(1)}) custom-call(bf16[512,1024]{1,0:T(8,128)(2,1)} %act.1, bf16[512,1792]{1,0:T(8,128)(2,1)} %grad.1), custom_call_target="tpu_custom_call" | custom-call | tf_op jit(solution)/shard_map/pallas_call | solution.py:637
  123.5 0.0 copy-done
  123.5 0.0 copy-start.1
  123.5 1.4 %multiply_add_fusion = f32[56,7168]{1,0:T(8,128)} fusion(bf16[56,7168]{1,0:T(8,128)(2,1)S(1)} %get-tuple-element.5, f32[56,7168]{1,0:T(8,128)S(1)} %copy-done), kind=kLoop, calls=%fused_computation | loop fusion | flops 1605632 | bytes 4014080 | tf_op jit(solution)/shard_map/add | solution.py:655
  124.8 0.0 copy-done.1
  124.8 0.9 multiply_add_fusion.1
Async XLA Ops:
  0.6 122.8 %copy-start = (f32[56,7168]{1,0:T(8,128)S(1)}, f32[56,7168]{1,0:T(8,128)}, u32[]{:S(2)}) copy-start(f32[56,7168]{1,0:T(8,128)} %param.7) | copy-start | bytes 4816900
  123.5 1.4 %copy-start.1 = (f32[32,4096]{1,0:T(8,128)S(1)}, f32[32,4096]{1,0:T(8,128)}, u32[]{:S(2)}) copy-start(f32[32,4096]{1,0:T(8,128)} %param.6) | copy-start | bytes 1572868

commit v7 on v6

--- a/solution.py
+++ b/solution.py
@@ -29,14 +29,6 @@
 
 def pieces_of(m, half):
     return [i for i, p in enumerate(PIECES) if p[0] == m and p[3] == half]
-
-
-def scoped(name, f):
-    def g(*a):
-        with jax.named_scope(name + "#" + "_".join(str(x) for x in a if isinstance(x, int))):
-            return f(*a)
-
-    return g
 
 
 def kernel(
@@ -85,21 +77,20 @@
     y_a, y_b = (h, z, flip1(y), tr, tc), (h, z, flip3(y), tr, tc)
     z_a, z_b = (h, flip1(z), y, tr, tc), (h, flip3(z), y, tr, tc)
 
-    def partner(d):
-        f = flip1 if d % 2 == 0 else flip3
-        on_y = is_n if d < 2 else 1 - is_n
-        return (
-            h,
-            on_y * z + (1 - on_y) * f(z),
-            on_y * f(y) + (1 - on_y) * y,
-            tr,
-            tc,
-        )
+    ORDER_N = ((0, 1, 2, 3), (1, 0, 3, 2))
+    ORDER_R = ((2, 3, 0, 1), (3, 2, 1, 0))
+    along = (y_a, y_b, z_a, z_b)
+
+    def partner(k, j):
+        pair = zip(along[ORDER_N[k][j]], along[ORDER_R[k][j]])
+        return tuple(b + is_n * (a - b) for a, b in pair)
 
     half_z = z // 2
     c_mine = z % 2
     apart = (half_z + tc) % 2
-    side = (c_mine + apart * shift[1] + (1 - apart) * shift[0]) % 2
+    place = is_n * (1 - shift[1])
+    side = (c_mine + apart * (place + shift[1]) + (1 - apart) * shift[0]) % 2
+    moved = apart * place
     mirrors = 1 - (1 - is_n) * (1 - apart)
     kind = is_n * (1 + apart)
     turned_rows = (
@@ -213,9 +204,9 @@
     yb = y // 2
     ya = (y + yb) % 2
 
-    def weight(d0, d1, k):
-        on0, on1 = 2 ** ((d0 - k) % 4), 2 ** ((d1 - k) % 4)
-        return on0 + (1 - is_n) * (on1 - on0)
+    def weight(d, k):
+        at_n, at_r = 2 ** ORDER_N[k].index(d), 2 ** ORDER_R[k].index(d)
+        return at_r + is_n * (at_n - at_r)
 
     def stream_copy(m, k, q, to):
         return remote(
@@ -232,7 +223,7 @@
             prox[m].at[q, :, lanes_of(m, k)],
             recx[m].at[q, :, lanes_of(m, k)],
             x_send.at[m, k],
-            x_recv.at[m, k, q],
+            x_recv.at[m, q],
             to,
         )
 
@@ -254,22 +245,23 @@
 
     def product(m, e, order):
         c = (order + odd) % 2 if e else order
-        value = dot(m, e, c, (c + shift[e]) % 2)
+        s = (c + shift[e]) % 2
+        value = dot(m, e, c, s)
         rows = value.shape[0] // 8
         block = (tc + e) % 2
-        rza = (c + block + za) % 2
+        rza = (c + (place if e else 0) + block + za) % 2
         rzb = (block + zb) % 2
         for yy in range(4):
             rya, ryb = bits_of(yy)
             for k in range(2):
-                q = rza * weight(2, 0, k) + rzb * weight(3, 1, k)
-                q = q + rya * weight(0, 2, k) + ryb * weight(1, 3, k)
+                q = rza * weight(2, k) + rzb * weight(3, k)
+                q = q + rya * weight(0, k) + ryb * weight(1, k)
                 first = (2 * yy + k) * rows
                 prod[m][k, q] = value[first : first + rows].astype(jnp.bfloat16)
 
                 @pl.when(q % 2 == 1)
                 def _(k=k, q=q):
-                    stream_copy(m, k, q, partner(k)).start()
+                    stream_copy(m, k, q, partner(k, 0)).start()
 
     EXTRA = ((y_a, y_b, z_a, z_b), (z_b, z_a, y_b, y_a))
 
@@ -305,13 +297,14 @@
     early_1 = 1 - is_n * h
 
     def group_of(k, q):
-        def bit(d0, d1):
-            at0, at1 = 2 ** ((d0 - k) % 4), 2 ** ((d1 - k) % 4)
-            return is_n * (q // at0 % 2) + (1 - is_n) * (q // at1 % 2)
-
-        block = (bit(3, 1) + zb) % 2
-        c = (bit(2, 0) + za + block) % 2
+        def bit(d):
+            at_n, at_r = 2 ** ORDER_N[k].index(d), 2 ** ORDER_R[k].index(d)
+            return is_n * (q // at_n % 2) + (1 - is_n) * (q // at_r % 2)
+
+        block = (bit(3) + zb) % 2
+        c = (bit(2) + za + block) % 2
         e = (block + tc) % 2
+        c = (c + e * place) % 2
         second = (c + odd) % 2
         return (1 - e) * c + e * (2 * second + (1 - second) * (1 - early_1))
 
@@ -320,7 +313,7 @@
             for p in parts:
                 stream_copy(m, k, p, core).wait_recv()
             prod[m][k, q] = total(prod[m], recv[m], k, q, parts).astype(jnp.bfloat16)
-            stream_copy(m, k, q, partner((j + k) % 4)).start()
+            stream_copy(m, k, q, partner(k, j)).start()
 
         def one(i, carry):
             q = i * 2 ** (j + 1) + 2**j
@@ -334,9 +327,12 @@
 
         lax.fori_loop(0, 2 ** (3 - j), one, 0)
 
+    def extra_arrived(m, parts):
+        for p in parts:
+            slot = recx[m].at[p]
+            remote(slot, slot, x_send.at[m, 0], x_recv.at[m, p], core).wait_recv()
+
     def total_extra(m, k, q, parts):
-        for p in parts:
-            extra_copy(m, k, p, core).wait_recv()
         value = prox[m][q, :, lanes_of(m, k)].astype(jnp.float32)
         for p in parts:
             value = value + recx[m][p, :, lanes_of(m, k)].astype(jnp.float32)
@@ -346,6 +342,7 @@
         def one(i, carry):
             q = i * 2 ** (j + 1) + 2**j
             parts = [q + 2**b for b in range(j)]
+            extra_arrived(m, parts)
             for k in range(2):
                 prox[m][q, :, lanes_of(m, k)] = total_extra(m, k, q, parts).astype(jnp.bfloat16)
                 extra_copy(m, k, q, EXTRA[k][j]).start()
@@ -362,7 +359,8 @@
         return pl.ds(first, half)
 
     def last_copy(m, k):
-        to = others[k]
+        _, _, _, a, b = (*others, x1)[k]
+        to = (h, z + moved * (flip1(z) - z), y, a, b)
         return remote(
             fin[m].at[2 * to[3] + to[4]],
             row[m].at[:, at(m, 2 * tr + tc, side)],
@@ -394,11 +392,10 @@
             turn[m].at[i], mir[m].at[kind, y], m_send.at[m], m_recv.at[m, kind], to
         )
 
-    def by_quarter(m, ref, value, s):
+    def by_quarter(m, ref, value):
         rows = value.shape[0] // 4
         for i in range(4):
             ref[m][i] = value[i * rows : (i + 1) * rows].astype(jnp.bfloat16)
-        row[m][:, at(m, 2 * tr + tc, s)] = ref[m][2 * tr + tc]
 
     def finish(m):
         parts = (1, 2, 4, 8)
@@ -408,9 +405,17 @@
         value = jnp.concatenate(
             [total(prod[m], recv[m], k, 0, parts) for k in range(2)], axis=0
         )
-        by_quarter(m, fin, value, side)
+        by_quarter(m, fin, value)
         for k in range(3):
             last_copy(m, k).start()
+
+        @pl.when(moved == 1)
+        def _():
+            last_copy(m, 3).start()
+
+        @pl.when(moved == 0)
+        def _():
+            row[m][:, at(m, 2 * tr + tc, side)] = fin[m][2 * tr + tc]
 
         @pl.when(mirrors == 1)
         def _():
@@ -433,6 +438,7 @@
     def finish_extra(m):
         @pl.when(is_n == 0)
         def _():
+            extra_arrived(m, (1, 2, 4, 8))
             value = jnp.concatenate(
                 [total_extra(m, k, 0, (1, 2, 4, 8)) for k in range(2)], axis=1
             )
@@ -474,6 +480,10 @@
         for k in range(3):
             last_copy(m, k).wait_recv()
 
+        @pl.when(moved == 1)
+        def _():
+            last_copy(m, 3).wait_recv()
+
         @pl.when(c_mine * (1 - keeps) + (1 - c_mine) * keeps == 0)
         def _():
             last_extra(m).wait_recv()
@@ -509,17 +519,6 @@
         @pl.when(is_n == 0)
         def _():
             product_extra(m)
-
-    step_a = scoped("step_a", step_a)
-    step_b = scoped("step_b", step_b)
-    products = scoped("products", products)
-    extras = scoped("extras", extras)
-    stage = scoped("stage", stage)
-    stage_extra = scoped("stage_extra", stage_extra)
-    finish = scoped("finish", finish)
-    finish_extra = scoped("finish_extra", finish_extra)
-    gather_rows = scoped("gather_rows", gather_rows)
-    send_turned = scoped("send_turned", send_turned)
 
     for copy in own:
         copy.wait()
@@ -552,11 +551,11 @@
     stage(GRAD, 3)
     stage_extra(GRAD, 3)
     stage(ACT, 2)
+    finish(GRAD)
+    send_turned(GRAD)
     stage_extra(ACT, 2)
-    finish(GRAD)
     stage(ACT, 3)
     stage_extra(ACT, 3)
-    send_turned(GRAD)
     finish_extra(GRAD)
     finish(ACT)
     send_turned(ACT)
@@ -564,45 +563,49 @@
     gather_rows(GRAD)
     gather_rows(ACT)
 
-    with jax.named_scope("drain"):
-        def sent(ref, sem):
-            pltpu.make_async_copy(ref, ref, sem).wait()
-
-        for m in (ACT, GRAD):
-            block = buf[m].at[1]
-            sent(block, a_send.at[m])
-
-            @pl.when(is_n == 1)
-            def _(m=m, block=block):
-                for k in (0, 1):
-                    sent(block, b_send.at[k, m])
-
-            @pl.when(is_n == 0)
-            def _(m=m, block=block):
-                for k in range(4):
-                    sent(block, d_send.at[k, m])
-                for k in range(2):
-                    sent(prox[m].at[pl.ds(1, 15), :, lanes_of(m, k)], x_send.at[m, k])
-
-                @pl.when(keeps == 0)
-                def _():
-                    last_extra(m).wait_send()
-
-                for count in (15, 16):
-
-                    @pl.when(keeps_turned == 16 - count)
-                    def _(count=count):
-                        sent(turx[m].at[pl.ds(0, count)], n_send.at[m])
-
+    def sent(ref, sem):
+        pltpu.make_async_copy(ref, ref, sem).wait()
+
+    for m in (ACT, GRAD):
+        block = buf[m].at[1]
+        sent(block, a_send.at[m])
+
+        @pl.when(is_n == 1)
+        def _(m=m, block=block):
+            for k in (0, 1):
+                sent(block, b_send.at[k, m])
+
+        @pl.when(is_n == 0)
+        def _(m=m, block=block):
+            for k in range(4):
+                sent(block, d_send.at[k, m])
             for k in range(2):
-                sent(prod[m].at[k, pl.ds(1, 15)], s_send.at[m, k])
-            sent(fin[m].at[pl.ds(0, 3)], f_send.at[m])
-
-            @pl.when(mirrors == 1)
-            def _(m=m):
-                sent(turn[m], m_send.at[m])
-
-            own_out(m).wait()
+                sent(prox[m].at[pl.ds(1, 15), :, lanes_of(m, k)], x_send.at[m, k])
+
+            @pl.when(keeps == 0)
+            def _():
+                last_extra(m).wait_send()
+
+            for count in (15, 16):
+
+                @pl.when(keeps_turned == 16 - count)
+                def _(count=count):
+                    sent(turx[m].at[pl.ds(0, count)], n_send.at[m])
+
+        for k in range(2):
+            sent(prod[m].at[k, pl.ds(1, 15)], s_send.at[m, k])
+        for count in (3, 4):
+
+            @pl.when(moved == count - 3)
+            def _(m=m, count=count):
+                sent(fin[m].at[pl.ds(0, count)], f_send.at[m])
+
+
+        @pl.when(mirrors == 1)
+        def _(m=m):
+            sent(turn[m], m_send.at[m])
+
+        own_out(m).wait()
 
 
 def sums(activations, gradients, rows_a, rows_g):
@@ -629,8 +632,8 @@
     dma = pltpu.SemaphoreType.DMA
     sems = [
         dma((2,)), dma((2,)), dma((n,)), dma((2, 2)), dma((2, n)), dma((4, 2)), dma((4, n)),
-        dma((2, 2)), dma((2, 2, 16)), dma((2, 2)), dma((2, 2, 16)),
-        dma((2,)), dma((2, 3)), dma((2,)), dma((2,)),
+        dma((2, 2)), dma((2, 2, 16)), dma((2, 2)), dma((2, 16)),
+        dma((2,)), dma((2, 4)), dma((2,)), dma((2,)),
         dma((2,)), dma((2, 3)), dma((2,)), dma((2,)), dma((2,)),
     ]
     anywhere = pl.BlockSpec(memory_space=pl.ANY)

time: 126 us -> 124 us (0.984)
  the two profiles are of different devices: /device:TPU:97 before, /device:TPU:121 now
where the time goes in v7:
time: 124 us
  Pallas kernels  121 us (98%)
  other arithmetic  2.23 us (2%)
    pallas_call x1, Pallas kernels, sums(): pl.pallas_call(kernel, out_shape=[jax.ShapeDtypeStruct((r, 4 * w), bf16)...  121 us

profile of v7, /device:TPU:121, one launch (start us, length us, event | category | flops | bytes accessed | tf_op | source)
XLA Modules:
  0.0 124.1 jit_solution(6613783135051626151)
XLA Ops:
  0.6 0.0 copy-start
  0.6 121.2 %shard_map.59 = (bf16[32,4096]{1,0:T(8,128)(2,1)S(1)}, bf16[56,7168]{1,0:T(8,128)(2,1)S(1)}) custom-call(bf16[512,1024]{1,0:T(8,128)(2,1)} %act.1, bf16[512,1792]{1,0:T(8,128)(2,1)} %grad.1), custom_call_target="tpu_custom_call" | custom-call | tf_op jit(solution)/shard_map/pallas_call | solution.py:640
  121.8 0.0 copy-done
  121.8 0.0 copy-start.1
  121.8 1.4 %multiply_add_fusion = f32[56,7168]{1,0:T(8,128)} fusion(bf16[56,7168]{1,0:T(8,128)(2,1)S(1)} %get-tuple-element.5, f32[56,7168]{1,0:T(8,128)S(1)} %copy-done), kind=kLoop, calls=%fused_computation | loop fusion | flops 1605632 | bytes 4014080 | tf_op jit(solution)/shard_map/add | solution.py:658
  123.2 0.0 copy-done.1
  123.2 0.9 multiply_add_fusion.1
Async XLA Ops:
  0.6 121.2 %copy-start = (f32[56,7168]{1,0:T(8,128)S(1)}, f32[56,7168]{1,0:T(8,128)}, u32[]{:S(2)}) copy-start(f32[56,7168]{1,0:T(8,128)} %param.7) | copy-start | bytes 4816900
  121.8 1.4 %copy-start.1 = (f32[32,4096]{1,0:T(8,128)S(1)}, f32[32,4096]{1,0:T(8,128)}, u32[]{:S(2)}) copy-start(f32[32,4096]{1,0:T(8,128)} %param.6) | copy-start | bytes 1572868

commit v8 on v7

--- a/solution.py
+++ b/solution.py
@@ -21,10 +21,11 @@
     (GRAD, 384, 256, 1),
     (GRAD, 640, 256, 1),
     (ACT, 0, 512, 0),
-    (ACT, 0, 512, 1),
+    (ACT, 0, 256, 1),
+    (ACT, 256, 256, 1),
 )
 AT_ONCE = (0, 1, 2)
-AFTER = {1: (3, 4), 4: (5, 6)}
+AFTER = {1: (3, 4), 4: (5, 6, 7)}
 
 
 def pieces_of(m, half):

time: 124 us -> 124 us (level)
  the two profiles are of different devices: /device:TPU:121 before, /device:TPU:1 now
where the time goes in v8:
time: 124 us; the launch traced here: 123 us
  Pallas kernels  120 us (97%)
  other arithmetic  2.23 us (2%)
    pallas_call x1, Pallas kernels, sums(): pl.pallas_call(kernel, out_shape=[jax.ShapeDtypeStruct((r, 4 * w), bf16)...  120 us

profile of v8, /device:TPU:1, one launch (start us, length us, event | category | flops | bytes accessed | tf_op | source)
XLA Modules:
  0.0 122.7 jit_solution(10984704260009265160)
XLA Ops:
  0.6 0.0 copy-start
  0.6 119.8 %shard_map.59 = (bf16[32,4096]{1,0:T(8,128)(2,1)S(1)}, bf16[56,7168]{1,0:T(8,128)(2,1)S(1)}) custom-call(bf16[512,1024]{1,0:T(8,128)(2,1)} %act.1, bf16[512,1792]{1,0:T(8,128)(2,1)} %grad.1), custom_call_target="tpu_custom_call" | custom-call | tf_op jit(solution)/shard_map/pallas_call | solution.py:641
  120.4 0.0 copy-done
  120.5 0.0 copy-start.1
  120.5 1.4 %multiply_add_fusion = f32[56,7168]{1,0:T(8,128)} fusion(bf16[56,7168]{1,0:T(8,128)(2,1)S(1)} %get-tuple-element.5, f32[56,7168]{1,0:T(8,128)S(1)} %copy-done), kind=kLoop, calls=%fused_computation | loop fusion | flops 1605632 | bytes 4014080 | tf_op jit(solution)/shard_map/add | solution.py:659
  121.8 0.0 copy-done.1
  121.8 0.9 multiply_add_fusion.1
Async XLA Ops:
  0.6 119.8 %copy-start = (f32[56,7168]{1,0:T(8,128)S(1)}, f32[56,7168]{1,0:T(8,128)}, u32[]{:S(2)}) copy-start(f32[56,7168]{1,0:T(8,128)} %param.7) | copy-start | bytes 4816900
  120.5 1.4 %copy-start.1 = (f32[32,4096]{1,0:T(8,128)S(1)}, f32[32,4096]{1,0:T(8,128)}, u32[]{:S(2)}) copy-start(f32[32,4096]{1,0:T(8,128)} %param.6) | copy-start | bytes 1572868

commit v9 on v8

--- a/solution.py
+++ b/solution.py
@@ -17,9 +17,9 @@
 PIECES = (
     (GRAD, 0, 512, 0),
     (GRAD, 512, 384, 0),
-    (GRAD, 0, 384, 1),
-    (GRAD, 384, 256, 1),
-    (GRAD, 640, 256, 1),
+    (GRAD, 0, 512, 1),
+    (GRAD, 512, 256, 1),
+    (GRAD, 768, 128, 1),
     (ACT, 0, 512, 0),
     (ACT, 0, 256, 1),
     (ACT, 256, 256, 1),

time: 124 us -> 124 us (level)
  no operation moved by 1% of the time
where the time goes in v9:
time: 124 us; the launch traced here: 122 us
  Pallas kernels  120 us (97%)
  other arithmetic  2.23 us (2%)
    pallas_call x1, Pallas kernels, sums(): pl.pallas_call(kernel, out_shape=[jax.ShapeDtypeStruct((r, 4 * w), bf16)...  120 us

profile of v9, /device:TPU:1, one launch (start us, length us, event | category | flops | bytes accessed | tf_op | source)
XLA Modules:
  0.0 122.4 jit_solution(11136356113740199881)
XLA Ops:
  0.6 0.0 copy-start
  0.6 119.5 %shard_map.59 = (bf16[32,4096]{1,0:T(8,128)(2,1)S(1)}, bf16[56,7168]{1,0:T(8,128)(2,1)S(1)}) custom-call(bf16[512,1024]{1,0:T(8,128)(2,1)} %act.1, bf16[512,1792]{1,0:T(8,128)(2,1)} %grad.1), custom_call_target="tpu_custom_call" | custom-call | tf_op jit(solution)/shard_map/pallas_call | solution.py:641
  120.2 0.0 copy-done
  120.2 0.0 copy-start.1
  120.2 1.4 %multiply_add_fusion = f32[56,7168]{1,0:T(8,128)} fusion(bf16[56,7168]{1,0:T(8,128)(2,1)S(1)} %get-tuple-element.5, f32[56,7168]{1,0:T(8,128)S(1)} %copy-done), kind=kLoop, calls=%fused_computation | loop fusion | flops 1605632 | bytes 4014080 | tf_op jit(solution)/shard_map/add | solution.py:659
  121.6 0.0 copy-done.1
  121.6 0.9 multiply_add_fusion.1
Async XLA Ops:
  0.6 119.6 %copy-start = (f32[56,7168]{1,0:T(8,128)S(1)}, f32[56,7168]{1,0:T(8,128)}, u32[]{:S(2)}) copy-start(f32[56,7168]{1,0:T(8,128)} %param.7) | copy-start | bytes 4816900
  120.2 1.4 %copy-start.1 = (f32[32,4096]{1,0:T(8,128)S(1)}, f32[32,4096]{1,0:T(8,128)}, u32[]{:S(2)}) copy-start(f32[32,4096]{1,0:T(8,128)} %param.6) | copy-start | bytes 1572868
